TPU v7x, 256 devices: a whole 4x4x8 slice. The times are simulated.
256 devices in a mesh: det: 4 (over y), tm: 64 (over x, z, core).
Axes of the slice: x: 4, y: 4, z: 8, core: 2. Of those that a mesh axis runs over, the one named last changes fastest.
Arguments:
- detector_data: float32 [1024, 65536], P('det', 'tm'), may hold values from -250 to 250
- templates: bfloat16 [8, 16, 65536], P(None, None, 'tm'), may hold values from -5 to 5
- wafer_of: int32 [1024], P('det'), may hold values from 0 to 7, as said below
- knee_freq: float32 [1024], P(('det', 'tm')), may hold values from 0.1 to 5
- white_level: float32 [1024], P(('det', 'tm')), may hold values from 0.5 to 5
- tile_id: int32 [1024, 65536], P(('det', 'tm')), may hold values from 0 to 15
- pixel_id: int32 [1024, 65536], P(('det', 'tm')), may hold values from 0 to 127
- tile_order: int32 [16], replicated, may hold values from 0 to 15, each once
Outputs:
- fit_amps: float32 [16, 1024], P(None, 'det')
- weighted_data: bfloat16 [1024, 65536], P(('det', 'tm'))
- sky_map: float32 [2048], P('tm')
- weight_map: float32 [2048], P('tm')
Inputs may be any that keep to these rules, and one draw needn't show every extreme that they name: `wafer_of`: the detectors of each aligned run of 128 share one wafer, and each wafer has exactly one such run.
All inputs are finite; a program needn't handle non-finite values.
Results may differ from a plain program's by a relative error of at most 0.0016.
Values sent between devices are 32-bit elements; how exact they have to be, the bound alone decides.
A program may use at most 64 MiB of HBM per device.

v0:
```python
import math

import jax
import jax.numpy as jnp
from jax import lax
from jax.sharding import PartitionSpec as P

PIX = 128


precise = lax.Precision.HIGHEST
sample_rate = 200.0


def invert_blocks(matrices):
    dimension = matrices.shape[-1]
    identity = jnp.broadcast_to(jnp.eye(dimension, dtype=matrices.dtype), matrices.shape)
    joined = jnp.concatenate([matrices, identity], axis=-1)
    for column in range(dimension):
        pivot_row = joined[:, column, :] / joined[:, column, column][:, None]
        factor = joined[:, :, column]
        joined = joined - factor[:, :, None] * pivot_row[:, None, :]
        joined = joined.at[:, column, :].set(pivot_row)
    return joined[:, :, dimension:]


def cosine_sine(first_len, second_len, modulus):
    first_ramp = jnp.arange(first_len, dtype=jnp.int32)
    second_ramp = jnp.arange(second_len, dtype=jnp.int32)
    wrapped = first_ramp[:, None] * second_ramp[None, :] % modulus
    phase_angle = 2.0 * math.pi / modulus * wrapped.astype(jnp.float32)
    return (jnp.cos(phase_angle), jnp.sin(phase_angle))


def forward_transform(blocks):
    full_length = blocks.shape[2]
    side_cols = 2 ** ((full_length.bit_length() - 1) // 2)
    side_rows = full_length // side_cols
    signal_grid = blocks.reshape(blocks.shape[1], side_rows, side_cols)
    cos_rows, sin_rows = cosine_sine(side_rows, side_rows, side_rows)
    cos_cols, sin_cols = cosine_sine(side_cols, side_cols, side_cols)
    turn_cos, turn_sin = cosine_sine(side_rows, side_cols, full_length)
    real_y = jnp.einsum("kn,dnm->dkm", cos_rows, signal_grid, precision=precise)
    imag_y = -jnp.einsum("kn,dnm->dkm", sin_rows, signal_grid, precision=precise)
    real_z = real_y * turn_cos + imag_y * turn_sin
    imag_z = imag_y * turn_cos - real_y * turn_sin
    real_x = jnp.einsum("dkm,mj->dkj", real_z, cos_cols, precision=precise) + jnp.einsum(
        "dkm,mj->dkj", imag_z, sin_cols, precision=precise
    )
    imag_x = jnp.einsum("dkm,mj->dkj", imag_z, cos_cols, precision=precise) - jnp.einsum(
        "dkm,mj->dkj", real_z, sin_cols, precision=precise
    )
    return (real_x, imag_x)


def inverse_transform(real_x, imag_x):
    side_rows = real_x.shape[1]
    side_cols = real_x.shape[2]
    full_length = side_rows * side_cols
    cos_rows, sin_rows = cosine_sine(side_rows, side_rows, side_rows)
    cos_cols, sin_cols = cosine_sine(side_cols, side_cols, side_cols)
    turn_cos, turn_sin = cosine_sine(side_rows, side_cols, full_length)
    real_u = jnp.einsum("dkj,jn->dkn", real_x, cos_cols, precision=precise) - jnp.einsum(
        "dkj,jn->dkn", imag_x, sin_cols, precision=precise
    )
    imag_u = jnp.einsum("dkj,jn->dkn", real_x, sin_cols, precision=precise) + jnp.einsum(
        "dkj,jn->dkn", imag_x, cos_cols, precision=precise
    )
    real_w = real_u * turn_cos - imag_u * turn_sin
    imag_w = real_u * turn_sin + imag_u * turn_cos
    output = jnp.einsum("nk,dkm->dnm", cos_rows, real_w, precision=precise) - jnp.einsum(
        "nk,dkm->dnm", sin_rows, imag_w, precision=precise
    )
    return (output / full_length).reshape(real_x.shape[0], full_length)


def spectral_grid(side_rows, side_cols, knee_freq, white_level):
    full_length = side_rows * side_cols
    row_ramp = jnp.arange(side_rows, dtype=jnp.int32)
    col_ramp = jnp.arange(side_cols, dtype=jnp.int32)
    bin_index = row_ramp[:, None] + side_rows * col_ramp[None, :]
    folded = jnp.minimum(bin_index, full_length - bin_index).astype(jnp.float32)
    frequency = folded * (sample_rate / full_length)
    squared = frequency * frequency
    return squared[None, :, :] / (
        white_level[:, None, None] * (squared[None, :, :] + knee_freq[:, None, None] ** 2)
    )


def shards(
    detector_data, templates, wafer_of, knee_freq, white_level, tile_id, pixel_id, tile_order
):
    row_count = detector_data.shape[0]
    time_local = detector_data.shape[1]
    wafer_count = templates.shape[0]
    mode_count = templates.shape[1]
    wide_templates = templates.astype(jnp.float32)
    flat_templates = wide_templates.reshape(wafer_count * mode_count, time_local)
    gram_part = jnp.einsum("wkt,wjt->wkj", wide_templates, wide_templates, precision=precise)
    projected = jnp.einsum("ct,rt->cr", flat_templates, detector_data, precision=precise)
    projected = projected.reshape(wafer_count, mode_count, row_count)
    wafer_hot = (wafer_of[None, :] == jnp.arange(wafer_count, dtype=jnp.int32)[:, None]).astype(
        jnp.float32
    )
    gram_matrix, projected_sum = lax.psum((gram_part, projected), "tm")
    solved = jnp.einsum(
        "wkj,wjr->wkr", invert_blocks(gram_matrix), projected_sum, precision=precise
    )
    fit_amps = jnp.einsum("wkr,wr->kr", solved, wafer_hot, precision=precise)
    coefficients = (wafer_hot[:, None, :] * fit_amps[None, :, :]).reshape(
        wafer_count * mode_count, row_count
    )
    fitted = jnp.einsum("cr,ct->rt", coefficients, flat_templates, precision=precise)
    residual = detector_data - fitted
    owners = lax.axis_size("tm")
    local_dets = row_count // owners
    stacked = residual.reshape(owners, local_dets, time_local)
    real_x, imag_x = forward_transform(
        lax.all_to_all(stacked, "tm", split_axis=0, concat_axis=2, tiled=True)
    )
    weight_grid = spectral_grid(real_x.shape[1], real_x.shape[2], knee_freq, white_level)
    filtered = inverse_transform(real_x * weight_grid, imag_x * weight_grid)
    weighted_data = filtered.astype(jnp.bfloat16)
    full_length = filtered.shape[1]
    inverse_white = (1.0 / white_level).astype(jnp.bfloat16)
    sample_weight = jnp.broadcast_to(inverse_white[:, None], weighted_data.shape).reshape(-1)
    value_flat = weighted_data.reshape(-1)
    tile_flat = tile_id.reshape(-1)
    pixel_flat = pixel_id.reshape(-1)
    cell_count = value_flat.shape[0]
    block_len = min(32768, cell_count)
    tile_count = tile_order.shape[0]
    tile_ramp = jnp.arange(tile_count, dtype=jnp.int32)
    pixel_ramp = jnp.arange(PIX, dtype=jnp.int32)

    def add_block(turn, totals):
        start = turn * block_len
        tiles_here = lax.dynamic_slice_in_dim(tile_flat, start, block_len)
        pixels_here = lax.dynamic_slice_in_dim(pixel_flat, start, block_len)
        values_here = lax.dynamic_slice_in_dim(value_flat, start, block_len)
        weights_here = lax.dynamic_slice_in_dim(sample_weight, start, block_len)
        tile_hot = (tiles_here[None, :] == tile_ramp[:, None]).astype(jnp.bfloat16)
        left_side = jnp.concatenate(
            [tile_hot * values_here[None, :], tile_hot * weights_here[None, :]], axis=0
        )
        pixel_hot = (pixels_here[:, None] == pixel_ramp[None, :]).astype(jnp.bfloat16)
        return totals + jnp.dot(left_side, pixel_hot, preferred_element_type=jnp.float32)

    totals = lax.fori_loop(
        0, cell_count // block_len, add_block, jnp.zeros((2 * tile_count, PIX), jnp.float32)
    )
    sky_part = totals[:tile_count][tile_order].reshape(-1)
    weight_part = totals[tile_count:][tile_order].reshape(-1)
    summed = lax.psum((sky_part, weight_part), "det")
    owned_sky, owned_weight = (
        lax.psum_scatter(summed[0], "tm", scatter_dimension=0, tiled=True),
        lax.psum_scatter(summed[1], "tm", scatter_dimension=0, tiled=True),
    )
    detector_total = local_dets * lax.axis_size("det") * owners
    scale = float(tile_count * PIX) / float(detector_total * full_length)
    return (fit_amps, weighted_data, owned_sky * scale, owned_weight * scale)


def solution(mesh):
    in_specs = (
        P("det", "tm"),
        P(None, None, "tm"),
        P("det"),
        P(("det", "tm")),
        P(("det", "tm")),
        P(("det", "tm"), None),
        P(("det", "tm"), None),
        P(),
    )
    out_specs = (P(None, "det"), P(("det", "tm"), None), P("tm"), P("tm"))
    return jax.shard_map(shards, mesh=mesh, in_specs=in_specs, out_specs=out_specs, check_vma=False)
```

profile of v0, /device:TPU:1, one launch (start us, length us, event | category | flops | bytes accessed | tf_op | source)
XLA Modules:
  0.0 716.3 jit_solution(18332346544325336458)
XLA Ops:
  7.2 0.9 copy-done
  8.1 2.6 fusion.24
  10.9 249.4 %psum.28 = f32[8,16,16]{2,1,0:T(8,128)S(1)} all-reduce(f32[8,16,16]{2,1,0:T(8,128)S(1)} %fusion.143), channel_id=1, replica_groups=mesh['det'=4,'tm'=64] {'tm'}, use_global_device_ids=true, to_apply=%region_0.0 | all-reduce | flops 2048 | bytes 16384 | tf_op jit(solution)/shard_map/psum | solution.py:105
  270.0 1.2 fusion.23
  271.9 1.3 reshape.810
  273.2 9.9 %all-to-all-start = ((f32[64,4,1024]{2,1,0:T(4,128)}), f32[64,4,1024]{2,1,0:T(4,128)S(1)}, u32[]{:S(2)}, u32[]{:S(2)}) async-start(f32[64,4,1024]{2,1,0:T(4,128)} %reshape.810), calls=%async_computation | async-start | bytes 2097152 | tf_op jit(solution)/shard_map/all_to_all | solution.py:119
  283.2 1.0 fusion.68
  284.3 1.0 fusion.67
  285.7 0.7 copy-done.2
  286.5 1.1 copy.70
  288.1 1.1 copy.73
  291.0 0.8 fusion.43
  291.8 19.7 %all-to-all-done = f32[64,4,1024]{2,1,0:T(4,128)S(1)} async-done(((f32[64,4,1024]{2,1,0:T(4,128)}), f32[64,4,1024]{2,1,0:T(4,128)S(1)}, u32[]{:S(2)}, u32[]{:S(2)}) %all-to-all-start) | async-done | bytes 1048608 | tf_op jit(solution)/shard_map/all_to_all | solution.py:119
  312.4 2.6 convolution_bitcast_fusion.1
  315.0 2.6 fusion.15
  317.7 2.8 fusion.53
  320.4 3.0 fusion.57
  323.4 3.0 fusion.18
  326.4 2.1 fusion.55
  328.5 2.1 fusion.45
  330.6 3.4 fusion.17
  333.9 2.1 convolution_subtract_fusion.1
  336.0 2.1 convolution_add_fusion
  338.1 2.0 fusion.29
  340.1 2.1 fusion.21
  342.4 1.2 copy.71
  343.6 111.1 %while.30 = (s32[]{:T(128)}, f32[32,128]{1,0:T(8,128)S(1)}, s32[262144]{0:T(1024)}, bf16[262144]{0:T(1024)(128)(2,1)}, bf16[262144]{0:T(1024)(128)(2,1)S(1)}, /*...) while((s32[]{:T(128)}, f32[32,128]{1,0:T(8,128)S(1)}, s32[262144]{0:T(1024)}, ...), condition=%wide.region_3.0_spmd.clone, body=%wide.region_2.0_spmd.clone.sunk | while | flops 278405120 | bytes 5406893 | solution.py:149
  343.6 0.9 dynamic_slice.37
  344.5 0.9 dynamic_slice.38
  345.7 0.9 dynamic_slice.36
  346.7 10.8 %fusion.160 = f32[32,128]{1,0:T(8,128)S(1)} fusion(s32[32768]{0:T(1024)S(1)} %dynamic_slice.36, bf16[16,32768]{1,0:T(8,128)(2,1)S(1)} %get-tuple-element.424, bf16[16,32768]{1,0:T(8,128)(2,1)S(1)} %get-tuple-element.425, f32[32,128]{1,0:T(8,128)S(1)} %get-tuple-element.437, pred[]{:T(512)S(6)} %compare.91), kind=kOutput, calls=%fused_computation.13.clone.1 | convolution fusion | flops 276832256 | bytes 2260993 | tf_op jit(solution)/shard_map/while/body/eval_jaxpr/dot_general | solution.py:147
  357.5 0.9 dynamic_slice.37
  358.4 0.9 dynamic_slice.38
  359.6 0.9 dynamic_slice.36
  360.6 10.8 %fusion.160 = f32[32,128]{1,0:T(8,128)S(1)} fusion(s32[32768]{0:T(1024)S(1)} %dynamic_slice.36, bf16[16,32768]{1,0:T(8,128)(2,1)S(1)} %get-tuple-element.424, bf16[16,32768]{1,0:T(8,128)(2,1)S(1)} %get-tuple-element.425, f32[32,128]{1,0:T(8,128)S(1)} %get-tuple-element.437, pred[]{:T(512)S(6)} %compare.91), kind=kOutput, calls=%fused_computation.13.clone.1 | convolution fusion | flops 276832256 | bytes 2260993 | tf_op jit(solution)/shard_map/while/body/eval_jaxpr/dot_general | solution.py:147
  371.4 0.9 dynamic_slice.37
  372.3 0.9 dynamic_slice.38
  373.5 0.9 dynamic_slice.36
  374.5 10.8 %fusion.160 = f32[32,128]{1,0:T(8,128)S(1)} fusion(s32[32768]{0:T(1024)S(1)} %dynamic_slice.36, bf16[16,32768]{1,0:T(8,128)(2,1)S(1)} %get-tuple-element.424, bf16[16,32768]{1,0:T(8,128)(2,1)S(1)} %get-tuple-element.425, f32[32,128]{1,0:T(8,128)S(1)} %get-tuple-element.437, pred[]{:T(512)S(6)} %compare.91), kind=kOutput, calls=%fused_computation.13.clone.1 | convolution fusion | flops 276832256 | bytes 2260993 | tf_op jit(solution)/shard_map/while/body/eval_jaxpr/dot_general | solution.py:147
  385.3 0.9 dynamic_slice.37
  386.2 0.9 dynamic_slice.38
  387.4 0.9 dynamic_slice.36
  388.4 10.8 %fusion.160 = f32[32,128]{1,0:T(8,128)S(1)} fusion(s32[32768]{0:T(1024)S(1)} %dynamic_slice.36, bf16[16,32768]{1,0:T(8,128)(2,1)S(1)} %get-tuple-element.424, bf16[16,32768]{1,0:T(8,128)(2,1)S(1)} %get-tuple-element.425, f32[32,128]{1,0:T(8,128)S(1)} %get-tuple-element.437, pred[]{:T(512)S(6)} %compare.91), kind=kOutput, calls=%fused_computation.13.clone.1 | convolution fusion | flops 276832256 | bytes 2260993 | tf_op jit(solution)/shard_map/while/body/eval_jaxpr/dot_general | solution.py:147
  399.2 0.9 dynamic_slice.37
  400.1 0.9 dynamic_slice.38
  401.3 0.9 dynamic_slice.36
  402.2 10.8 %fusion.160 = f32[32,128]{1,0:T(8,128)S(1)} fusion(s32[32768]{0:T(1024)S(1)} %dynamic_slice.36, bf16[16,32768]{1,0:T(8,128)(2,1)S(1)} %get-tuple-element.424, bf16[16,32768]{1,0:T(8,128)(2,1)S(1)} %get-tuple-element.425, f32[32,128]{1,0:T(8,128)S(1)} %get-tuple-element.437, pred[]{:T(512)S(6)} %compare.91), kind=kOutput, calls=%fused_computation.13.clone.1 | convolution fusion | flops 276832256 | bytes 2260993 | tf_op jit(solution)/shard_map/while/body/eval_jaxpr/dot_general | solution.py:147
  413.1 0.9 dynamic_slice.37
  414.0 0.9 dynamic_slice.38
  415.2 0.9 dynamic_slice.36
  416.1 10.8 %fusion.160 = f32[32,128]{1,0:T(8,128)S(1)} fusion(s32[32768]{0:T(1024)S(1)} %dynamic_slice.36, bf16[16,32768]{1,0:T(8,128)(2,1)S(1)} %get-tuple-element.424, bf16[16,32768]{1,0:T(8,128)(2,1)S(1)} %get-tuple-element.425, f32[32,128]{1,0:T(8,128)S(1)} %get-tuple-element.437, pred[]{:T(512)S(6)} %compare.91), kind=kOutput, calls=%fused_computation.13.clone.1 | convolution fusion | flops 276832256 | bytes 2260993 | tf_op jit(solution)/shard_map/while/body/eval_jaxpr/dot_general | solution.py:147
  427.0 0.9 dynamic_slice.37
  427.9 0.9 dynamic_slice.38
  429.1 0.9 dynamic_slice.36
  430.0 10.8 %fusion.160 = f32[32,128]{1,0:T(8,128)S(1)} fusion(s32[32768]{0:T(1024)S(1)} %dynamic_slice.36, bf16[16,32768]{1,0:T(8,128)(2,1)S(1)} %get-tuple-element.424, bf16[16,32768]{1,0:T(8,128)(2,1)S(1)} %get-tuple-element.425, f32[32,128]{1,0:T(8,128)S(1)} %get-tuple-element.437, pred[]{:T(512)S(6)} %compare.91), kind=kOutput, calls=%fused_computation.13.clone.1 | convolution fusion | flops 276832256 | bytes 2260993 | tf_op jit(solution)/shard_map/while/body/eval_jaxpr/dot_general | solution.py:147
  440.9 0.9 dynamic_slice.37
  441.8 0.9 dynamic_slice.38
  443.0 0.9 dynamic_slice.36
  443.9 10.8 %fusion.160 = f32[32,128]{1,0:T(8,128)S(1)} fusion(s32[32768]{0:T(1024)S(1)} %dynamic_slice.36, bf16[16,32768]{1,0:T(8,128)(2,1)S(1)} %get-tuple-element.424, bf16[16,32768]{1,0:T(8,128)(2,1)S(1)} %get-tuple-element.425, f32[32,128]{1,0:T(8,128)S(1)} %get-tuple-element.437, pred[]{:T(512)S(6)} %compare.91), kind=kOutput, calls=%fused_computation.13.clone.1 | convolution fusion | flops 276832256 | bytes 2260993 | tf_op jit(solution)/shard_map/while/body/eval_jaxpr/dot_general | solution.py:147
  454.8 0.7 gather_fusion
  455.5 0.7 gather_fusion.1
  456.1 242.6 %all-reduce.2 = (f32[2048]{0:T(1024)S(1)}, f32[2048]{0:T(1024)S(1)}) all-reduce(f32[2048]{0:T(1024)S(1)} %bitcast.120, f32[2048]{0:T(1024)S(1)} %bitcast.121), channel_id=2, replica_groups=mesh['det'=4,'tm'=64] {'tm'}, use_global_device_ids=true, to_apply=%region_5.0.clone | all-reduce | flops 4096 | bytes 32768
  698.9 1.2 copy.69
  700.1 8.7 %all-reduce.3 = (f32[32]{0:T(128)S(1)}, f32[32]{0:T(128)S(1)}) all-reduce(f32[32]{0:T(128)S(1)} %dynamic-slice.129, f32[32]{0:T(128)S(1)} %dynamic-slice.131), channel_id=1, replica_groups=mesh['det'=4,'tm'=64] {'det'}, use_global_device_ids=true, to_apply=%region_4.0 | all-reduce | flops 64 | bytes 512 | tf_op jit(solution)/shard_map/psum | solution.py:154
  (142 shorter events, 16.9 us)
Async XLA Ops:
  7.2 1.0 copy-start
  7.2 262.8 %all-reduce.6.cloned.1.call-start = ((), (), s32[]{:S(2)}) async-start(), calls=%async_computation.1 | async-start | bytes 262144 | tf_op jit(solution)/shard_map/psum | solution.py:105
  264.5 5.4 copy-start.6
  265.3 5.9 copy-start.1
  271.2 0.7 copy-start.5
  273.2 38.3 %all-to-all-start = ((f32[64,4,1024]{2,1,0:T(4,128)}), f32[64,4,1024]{2,1,0:T(4,128)S(1)}, u32[]{:S(2)}, u32[]{:S(2)}) async-start(f32[64,4,1024]{2,1,0:T(4,128)} %reshape.810), calls=%async_computation | async-start | bytes 2097152 | tf_op jit(solution)/shard_map/all_to_all | solution.py:119
  283.1 2.3 copy-start.7
  283.1 2.3 copy-start.9
  285.2 1.2 copy-start.2
  286.5 1.6 copy-start.3
  288.1 1.1 copy-start.10
  288.1 2.3 copy-start.8
  320.4 3.0 copy-start.4
Sparse Core Ops, SparseCore 0:
  12.0 180.1 all-reduce.5
where the time goes:
time: 726 us; the launch traced here: 716 us
  blocking collectives  501 us (69%)
  matrix products  121 us (17%)
  local copies, waits for them, and re-layouts  39.8 us (5%)
  waiting for transfers between devices  19.8 us (3%)
  between operations  15.6 us (2%)
  starting transfers between devices  9.95 us (1%)
  other arithmetic  9.2 us (1%)
    psum x1, blocking collectives, shards(): gram_matrix, projected_sum = lax.psum((gram_part, projected), 'tm')  249 us
    unnamed x1, blocking collectives  243 us
    dot_general x8, matrix products, add_block(): jnp.dot(left_side, pixel_hot, preferred_element_type=jnp.float32)  86.5 us
    all_to_all x1, waiting for transfers between devices, shards(): lax.all_to_all(stacked, 'tm', split_axis=0, concat_axis=2, tiled=True)  19.7 us
  transfers between devices with their start and end apart: 2, of which 1 were waited for; matrix products, arithmetic and copies ran while one was open for 2% of the time, Pallas kernels for 0%

commit v1 on v0

v1 whole, which is shorter than its diff:
```python
import functools
import math

import jax
import jax.numpy as jnp
import numpy as np
from jax import lax
from jax.experimental import pallas as pl
from jax.experimental.pallas import tpu as pltpu
from jax.sharding import PartitionSpec as P

PIX = 128
MODES = 16
LANES = 128
SIDE = 256
HALF = SIDE // 2
ROWS = HALF + 8
sample_rate = 200.0
f32 = jnp.float32
bf16 = jnp.bfloat16
MESH = pl.DeviceIdType.MESH
NT = (((1,), (1,)), ((), ()))
NN = (((1,), (0,)), ((), ()))


def mm(a, b, dims=NN):
    return lax.dot_general(a, b, dims, preferred_element_type=f32)


def split2(x):
    high = x.astype(bf16)
    low = (x - high.astype(f32)).astype(bf16)
    return high, low


def split3(x):
    high = x.astype(bf16)
    rest = x - high.astype(f32)
    mid = rest.astype(bf16)
    low = (rest - mid.astype(f32)).astype(bf16)
    return high, mid, low


def fit_kernel(
    sizes, wafer_ref, data_ref, templates_ref, amps_ref, out_ref,
    parts, from_core, x_slots, z_slots, both, core_send, core_recv, x_send, x_recv, z_send, z_recv
):
    x_size, z_size = sizes
    tm = lax.axis_index("tm")
    core = tm % 2
    z = (tm // 2) % z_size
    x = tm // (2 * z_size)

    def index_of(x_at, z_at, core_at):
        return (x_at * z_size + z_at) * 2 + core_at

    other = index_of(x, z, 1 - core)
    x_peers = [index_of((x + k) % x_size, z, core) for k in range(1, x_size)]
    z_peers = [index_of(x, (z + k) % z_size, core) for k in range(1, z_size)]
    peers = [other] + x_peers + z_peers
    barrier = pltpu.get_barrier_semaphore()
    for peer in peers:
        pl.semaphore_signal(barrier, inc=1, device_id={"tm": peer}, device_id_type=MESH)

    run = data_ref.shape[0] // 2
    shapes = []
    for w in range(2):
        shape = templates_ref[wafer_ref[w * run]]
        shapes.append(shape)
        high, mid, low = split3(data_ref[w * run : (w + 1) * run, :])
        projected = mm(shape, high, NT) + mm(shape, mid, NT) + mm(shape, low, NT)
        gram = mm(shape, shape, NT)
        parts[w, 0:MODES, :] = projected
        pad = jnp.zeros((8, LANES - 2 * MODES), f32)
        parts[w, MODES : MODES + 8, :] = jnp.concatenate([gram[0:8], gram[8:16], pad], axis=1)

    pl.semaphore_wait(barrier, len(peers))
    copy = pltpu.make_async_remote_copy(
        src_ref=parts.at[1 - core], dst_ref=from_core, send_sem=core_send.at[0], recv_sem=core_recv.at[0],
        device_id={"tm": other}, device_id_type=MESH,
    )
    copy.start()
    copy.wait()
    mine = parts[core] + from_core[...]

    def exchange(mine, slots, place, peers, send_sem, recv_sem):
        slots[place] = mine
        copies = []
        for k, peer in enumerate(peers):
            copy = pltpu.make_async_remote_copy(
                src_ref=slots.at[place], dst_ref=slots.at[place], send_sem=send_sem.at[k], recv_sem=recv_sem.at[k],
                device_id={"tm": peer}, device_id_type=MESH,
            )
            copy.start()
            copies.append(copy)
        for copy in copies:
            copy.wait()
        total = slots[0]
        for k in range(1, len(peers) + 1):
            total = total + slots[k]
        return total

    mine = exchange(mine, x_slots, x, x_peers, x_send, x_recv)
    mine = exchange(mine, z_slots, z, z_peers, z_send, z_recv)
    both[core] = mine
    copy = pltpu.make_async_remote_copy(
        src_ref=both.at[core], dst_ref=both.at[core], send_sem=core_send.at[1], recv_sem=core_recv.at[1],
        device_id={"tm": other}, device_id_type=MESH,
    )
    copy.start()
    copy.wait()

    row = lax.broadcasted_iota(jnp.int32, (1, MODES, LANES), 1)
    for w in range(2):
        packed = both[w, MODES : MODES + 8, :]
        columns = []
        for k in range(MODES):
            top = jnp.broadcast_to(packed[:, k : k + 1], (8, LANES))
            low = jnp.broadcast_to(packed[:, MODES + k : MODES + k + 1], (8, LANES))
            columns.append(jnp.concatenate([top, low], axis=0))
        columns.append(both[w, 0:MODES, :])
        joined = jnp.stack(columns, axis=0)
        for c in range(MODES):
            factor = joined[0:1]
            pivot_row = joined[1:, c : c + 1, :] / factor[:, c : c + 1, :]
            joined = jnp.where(row == c, pivot_row, joined[1:] - factor * pivot_row)
        amps = joined[0]
        amps_ref[:, w * run : (w + 1) * run] = amps
        high, mid, low = split3(amps)
        left = jnp.concatenate([high, mid, low], axis=0)
        right = jnp.concatenate([shapes[w]] * 3, axis=0)
        fitted = lax.dot_general(left, right, (((0,), (0,)), ((), ())), preferred_element_type=f32)
        residual = data_ref[w * run : (w + 1) * run, :] - fitted
        tiles = residual.shape[1] // LANES
        for l in range(tiles):
            out_ref[pl.ds(w * run * tiles + l, run, stride=tiles), :] = residual[:, l * LANES : (l + 1) * LANES]


def fit(mesh, detector_data, templates, wafer_of):
    rows, local = detector_data.shape
    x_size, z_size = 4, 8
    part = (MODES + 8, LANES)
    return pl.pallas_call(
        functools.partial(fit_kernel, (x_size, z_size)),
        out_shape=(
            jax.ShapeDtypeStruct((MODES, rows), f32),
            jax.ShapeDtypeStruct((rows * local // LANES, LANES), f32),
        ),
        in_specs=[
            pl.BlockSpec(memory_space=pltpu.SMEM),
            pl.BlockSpec(memory_space=pltpu.VMEM),
            pl.BlockSpec(memory_space=pltpu.VMEM),
        ],
        out_specs=[pl.BlockSpec(memory_space=pltpu.VMEM)] * 2,
        scratch_shapes=[
            pltpu.VMEM((2,) + part, f32),
            pltpu.VMEM(part, f32),
            pltpu.VMEM((x_size,) + part, f32),
            pltpu.VMEM((z_size,) + part, f32),
            pltpu.VMEM((2,) + part, f32),
            pltpu.SemaphoreType.DMA((2,)),
            pltpu.SemaphoreType.DMA((2,)),
            pltpu.SemaphoreType.DMA((x_size - 1,)),
            pltpu.SemaphoreType.DMA((x_size - 1,)),
            pltpu.SemaphoreType.DMA((z_size - 1,)),
            pltpu.SemaphoreType.DMA((z_size - 1,)),
        ],
        compiler_params=pltpu.CompilerParams(collective_id=0, has_side_effects=True),
        name="fit",
    )(wafer_of, detector_data, templates)


CHUNK = 2048


def cell_hots(tile_ref, pixel_ref, start, values=None):
    span = pl.ds(pl.multiple_of(start, CHUNK), CHUNK)
    tiles = tile_ref[:, span]
    pixels = pixel_ref[:, span]
    left_id = (tiles + 16 * (pixels >> 6)).astype(f32).astype(bf16)
    right_id = (pixels & 63).astype(f32).astype(bf16)
    return left_id, right_id


def counts_kernel(tile_ref, pixel_ref, white_ref, out_ref):
    dets, samples = tile_ref.shape
    left_ramp = lax.broadcasted_iota(jnp.int32, (32, CHUNK), 0).astype(f32).astype(bf16)
    right_ramp = lax.broadcasted_iota(jnp.int32, (64, CHUNK), 0).astype(f32).astype(bf16)
    one, zero = jnp.ones((), bf16), jnp.zeros((), bf16)

    def step(turn, totals):
        left_id, right_id = cell_hots(tile_ref, pixel_ref, turn * CHUNK)
        fresh = []
        for d in range(dets):
            left = jnp.where(left_id[d : d + 1] == left_ramp, one, zero)
            right = jnp.where(right_id[d : d + 1] == right_ramp, one, zero)
            fresh.append(totals[d] + mm(left, right, NT))
        return tuple(fresh)

    totals = lax.fori_loop(0, samples // CHUNK, step, (jnp.zeros((32, 64), f32),) * dets)
    total = jnp.zeros((32, 64), f32)
    for d in range(dets):
        inverse = (jnp.ones((1, 64), f32) / jnp.full((1, 64), white_ref[d], f32)).astype(bf16).astype(f32)
        total = total + totals[d] * inverse
    out_ref[...] = jnp.concatenate([total[0:16], total[16:32]], axis=1)


def counts(tile_id, pixel_id, white_level):
    vmem = pl.BlockSpec(memory_space=pltpu.VMEM)
    return pl.pallas_call(
        counts_kernel,
        out_shape=jax.ShapeDtypeStruct((16, LANES), f32),
        in_specs=[vmem, vmem, pl.BlockSpec(memory_space=pltpu.SMEM)],
        out_specs=vmem,
        cost_estimate=pl.CostEstimate(flops=10**10, bytes_accessed=2**21, transcendentals=0),
        name="counts",
    )(tile_id, pixel_id, white_level)


def tables(chunks):
    full = SIDE * SIDE
    per = SIDE // chunks
    ramp = np.arange(SIDE)
    order = np.array([per * s + j for j in range(per) for s in range(chunks)])
    angle = 2.0 * np.pi / SIDE * (np.outer(ramp, ramp) % SIDE)
    cos, sin = np.cos(angle), np.sin(angle)
    first = np.concatenate([cos[:HALF], -sin[:HALF]], axis=0)
    first[HALF] = cos[HALF]
    second = np.block([[cos, -sin], [sin, cos]])
    weight = np.full((HALF,), 2.0)
    weight[0] = 1.0
    last = np.concatenate([cos[:, :HALF] * weight, -sin[:, :HALF] * weight], axis=1)
    last[:, HALF] = cos[:, HALF]
    k = np.arange(ROWS)
    turn = 2.0 * np.pi / full * np.outer(k, ramp)
    valid = (k <= HALF)[:, None]
    turn_cos, turn_sin = np.cos(turn) * valid, np.sin(turn) * valid
    bins = k[:, None] + SIDE * ramp[None, :]
    folded = np.minimum(bins, full - bins).astype(np.float32)
    frequency = folded * np.float32(sample_rate / full)
    squared = np.where(valid, frequency * frequency, np.float32(0)).astype(np.float32)

    def halves(a):
        a = a.astype(np.float32)
        high = a.astype(jnp.bfloat16)
        return high, (a - high.astype(np.float32)).astype(jnp.bfloat16)

    return (
        *halves(first[:, order]),
        *halves(second),
        *halves(last / full),
        turn_cos.astype(np.float32),
        turn_sin.astype(np.float32),
        squared,
    )


def three(left, right, dims=NN):
    return mm(left[0], right[0], dims) + mm(left[0], right[1], dims) + mm(left[1], right[0], dims)


def filter_kernel(
    scale, knee_ref, white_ref, order_ref, data_ref, tile_ref, pixel_ref, weight_ref,
    first_high, first_low, second_high, second_low, last_high, last_low, turn_cos, turn_sin, squared_ref,
    weighted_ref, maps_ref,
    flat, comb, tm_slots, det_slots, tm_send, tm_recv, det_send, det_recv
):
    dets = tile_ref.shape[0]
    samples = tile_ref.shape[1]
    owners = tm_slots.shape[0]
    det_size = det_slots.shape[0]
    tm = lax.axis_index("tm")
    det = lax.axis_index("det")
    barrier = pltpu.get_barrier_semaphore()

    def greet(k, carry):
        pl.semaphore_signal(barrier, inc=1, device_id={"tm": (tm + k) % owners}, device_id_type=MESH)
        return carry

    lax.fori_loop(1, owners, greet, 0)
    for k in range(1, det_size):
        pl.semaphore_signal(barrier, inc=1, device_id={"det": (det + k) % det_size}, device_id_type=MESH)

    chunks = owners
    per = SIDE // chunks
    tiles = SIDE // LANES
    block = per * tiles
    for d in range(dets):
        rows = []
        for j in range(per):
            rows.append(
                jnp.concatenate(
                    [
                        data_ref[pl.ds(d * block + j * tiles + h, chunks, stride=dets * block), :]
                        for h in range(tiles)
                    ],
                    axis=1,
                )
            )
        signal = jnp.concatenate(rows, axis=0)
        spectrum = three((first_high[...], first_low[...]), split2(signal))
        real_y, imag_y, tail = spectrum[0:HALF], spectrum[HALF:], spectrum[HALF : HALF + 8]
        first_row = lax.broadcasted_iota(jnp.int32, (HALF, SIDE), 0) == 0
        imag_y = jnp.where(first_row, 0.0, imag_y)
        cos_main, sin_main = turn_cos[0:HALF, :], turn_sin[0:HALF, :]
        cos_tail, sin_tail = turn_cos[HALF:, :], turn_sin[HALF:, :]
        real_z = jnp.concatenate([real_y * cos_main + imag_y * sin_main, tail * cos_tail], axis=0)
        imag_z = jnp.concatenate([imag_y * cos_main - real_y * sin_main, -tail * sin_tail], axis=0)
        bins = three(
            split2(jnp.concatenate([real_z, imag_z], axis=1)), (second_high[...], second_low[...])
        )
        squared = squared_ref[...]
        knee = knee_ref[d]
        gain = squared / (white_ref[d] * (squared + knee * knee))
        bins = bins * jnp.concatenate([gain, gain], axis=1)
        back = three(split2(bins), (second_high[...], second_low[...]), NT)
        real_u, imag_u = back[:, 0:SIDE], back[:, SIDE:]
        real_w = real_u[0:HALF] * cos_main - imag_u[0:HALF] * sin_main
        imag_w = real_u[0:HALF] * sin_main + imag_u[0:HALF] * cos_main
        tail_w = (real_u[HALF:] * cos_tail - imag_u[HALF:] * sin_tail)[0:1]
        imag_w = jnp.where(first_row, jnp.broadcast_to(tail_w, (HALF, SIDE)), imag_w)
        joined = jnp.concatenate([real_w, imag_w], axis=0)
        output = three((last_high[...], last_low[...]), split2(joined))
        for h in range(tiles):
            flat[pl.ds(h * dets + d, SIDE, stride=tiles * dets), :] = output[:, h * LANES : (h + 1) * LANES]
    weighted_ref[...] = flat[...].astype(bf16)

    left_ramp = lax.broadcasted_iota(jnp.int32, (32, CHUNK), 0).astype(f32).astype(bf16)
    right_ramp = lax.broadcasted_iota(jnp.int32, (64, CHUNK), 0).astype(f32).astype(bf16)
    one, zero = jnp.ones((), bf16), jnp.zeros((), bf16)

    def step(turn, total):
        left_id, right_id = cell_hots(tile_ref, pixel_ref, turn * CHUNK)
        width = CHUNK // LANES * dets
        values = flat[pl.ds(pl.multiple_of(turn * width, width), width), :].astype(bf16)
        for d in range(dets):
            value = jnp.concatenate(
                [values[l * dets + d : l * dets + d + 1, :] for l in range(CHUNK // LANES)], axis=1
            )
            left = jnp.where(left_id[d : d + 1] == left_ramp, value, zero)
            right = jnp.where(right_id[d : d + 1] == right_ramp, one, zero)
            total = total + mm(left, right, NT)
        return total

    total = lax.fori_loop(0, samples // CHUNK, step, jnp.zeros((32, 64), f32))
    comb[0] = jnp.concatenate([total[0:16], total[16:32]], axis=1)
    comb[1] = weight_ref[...]

    ordered = tm_slots.shape
    del ordered
    for r in range(16):
        tile = order_ref[r]
        maps_ref[r, 0:1, :] = comb[0, pl.ds(tile, 1), :]
        maps_ref[r, 1:2, :] = comb[1, pl.ds(tile, 1), :]
    share = owners // 16

    pl.semaphore_wait(barrier, owners - 1 + det_size - 1)

    def send(k, carry):
        peer = (tm + k) % owners
        pltpu.make_async_remote_copy(
            src_ref=maps_ref.at[peer // share], dst_ref=tm_slots.at[tm], send_sem=tm_send, recv_sem=tm_recv,
            device_id={"tm": peer}, device_id_type=MESH,
        ).start()
        return carry

    lax.fori_loop(1, owners, send, 0)
    tm_slots[tm] = maps_ref[tm // share]
    everything = pltpu.make_async_remote_copy(
        src_ref=tm_slots.at[pl.ds(0, owners - 1)], dst_ref=tm_slots.at[pl.ds(0, owners - 1)],
        send_sem=tm_send, recv_sem=tm_recv, device_id={"tm": (tm + 1) % owners}, device_id_type=MESH,
    )
    everything.wait()
    det_slots[det] = jnp.sum(tm_slots[...], axis=0)
    copies = []
    for k in range(1, det_size):
        copy = pltpu.make_async_remote_copy(
            src_ref=det_slots.at[det], dst_ref=det_slots.at[det], send_sem=det_send.at[k - 1],
            recv_sem=det_recv.at[k - 1], device_id={"det": (det + k) % det_size}, device_id_type=MESH,
        )
        copy.start()
        copies.append(copy)
    for copy in copies:
        copy.wait()
    total = det_slots[0]
    for k in range(1, det_size):
        total = total + det_slots[k]
    maps_ref[0] = total * scale


def weigh(scale, det_size, owners, knee_freq, white_level, tile_order, data, tile_id, pixel_id, weight_part):
    dets, samples = tile_id.shape
    vmem = pl.BlockSpec(memory_space=pltpu.VMEM)
    smem = pl.BlockSpec(memory_space=pltpu.SMEM)
    factors = tables(owners)
    return pl.pallas_call(
        functools.partial(filter_kernel, scale),
        out_shape=(
            jax.ShapeDtypeStruct((dets * samples // LANES, LANES), bf16),
            jax.ShapeDtypeStruct((16, 2, LANES), f32),
        ),
        in_specs=[smem] * 3 + [vmem] * (4 + len(factors)),
        out_specs=[vmem] * 2,
        scratch_shapes=[
            pltpu.VMEM((dets * samples // LANES, LANES), f32),
            pltpu.VMEM((2, 16, LANES), f32),
            pltpu.VMEM((owners, 2, LANES), f32),
            pltpu.VMEM((det_size, 2, LANES), f32),
            pltpu.SemaphoreType.DMA,
            pltpu.SemaphoreType.DMA,
            pltpu.SemaphoreType.DMA((det_size - 1,)),
            pltpu.SemaphoreType.DMA((det_size - 1,)),
        ],
        compiler_params=pltpu.CompilerParams(collective_id=1, has_side_effects=True),
        name="weigh",
    )(knee_freq, white_level, tile_order, data, tile_id, pixel_id, weight_part, *factors)


def shards(
    mesh, detector_data, templates, wafer_of, knee_freq, white_level, tile_id, pixel_id, tile_order
):
    owners = mesh.shape["tm"]
    det_size = mesh.shape["det"]
    dets, samples = tile_id.shape
    fit_amps, residual = fit(mesh, detector_data, templates, wafer_of)
    rows = residual.shape[0] // owners
    moved = lax.all_to_all(residual.reshape(owners, rows, LANES), "tm", split_axis=0, concat_axis=0, tiled=True)
    moved = moved.reshape(owners * rows, LANES)
    weight_part = counts(tile_id, pixel_id, white_level)
    cells = 16 * PIX
    scale = float(cells) / float(dets * owners * det_size * samples)
    weighted, maps = weigh(
        scale, det_size, owners, knee_freq, white_level, tile_order, moved, tile_id, pixel_id, weight_part
    )
    weighted = weighted.reshape(samples // LANES, dets, LANES).transpose(1, 0, 2).reshape(dets, samples)
    share = cells // owners
    start = (lax.axis_index("tm") % (PIX // share)) * share
    own = lax.dynamic_slice(maps[0], (0, start), (2, share))
    return (fit_amps, weighted, own[0], own[1])


def solution(mesh):
    in_specs = (
        P("det", "tm"),
        P(None, None, "tm"),
        P("det"),
        P(("det", "tm")),
        P(("det", "tm")),
        P(("det", "tm"), None),
        P(("det", "tm"), None),
        P(),
    )
    out_specs = (P(None, "det"), P(("det", "tm"), None), P("tm"), P("tm"))
    return jax.shard_map(
        functools.partial(shards, mesh), mesh=mesh, in_specs=in_specs, out_specs=out_specs, check_vma=False
    )
```

time: 726 us -> 98.4 us (0.14); the launches traced: 716 us -> 98.1 us
  blocking collectives: 501 us -> 0 us
  matrix products: 121 us -> 0 us
  Pallas kernels: 0 us -> 72.8 us
  local copies, waits for them, and re-layouts: 39.8 us -> 4.86 us
  between operations: 15.6 us -> 0.68 us
  other arithmetic: 9.2 us -> 0 us
    psum x2 -> x0, blocking collectives: 258 us -> none  [the longest x1 249 us: shards(): gram_matrix, projected_sum = lax.psum((gram_part, projected), 'tm')]
    unnamed x1 -> x0, blocking collectives: 243 us -> none
    dot_general x24 -> x0, matrix products: 121 us -> none  [the longest x8 86.5 us: add_block(): jnp.dot(left_side, pixel_hot, preferred_element_type=jnp.float32)]
    pallas_call x0 -> x3, Pallas kernels: none -> 72.8 us  [the longest x1 34.6 us: weigh(): pl.pallas_call(functools.partial(filter_kernel, scale), out_shape=(jax.Sh...]
    dynamic_slice x32 -> x1, local copies, waits for them, and re-layouts: 21.5 us -> 0.07 us  [shards(): own = lax.dynamic_slice(maps[0], (0, start), (2, share))]
  transfers between devices with their start and end apart: 2 -> 1, of which waited for: 1 -> 1; matrix products, arithmetic and copies ran while one was open for 2% -> 0% of each run, Pallas kernels for 0% -> 16%
where the time goes in v1:
time: 98.4 us; the launch traced here: 98.1 us
  Pallas kernels  72.8 us (74%)
  waiting for transfers between devices  12.9 us (13%)
  starting transfers between devices  6.93 us (7%)
  local copies, waits for them, and re-layouts  4.86 us (5%)
    pallas_call x1, Pallas kernels, weigh(): pl.pallas_call(functools.partial(filter_kernel, scale), out_shape=(jax.Sh...  34.6 us
    pallas_call x1, Pallas kernels, fit(): pl.pallas_call(functools.partial(fit_kernel, (x_size, z_size)), out_shape...  22.6 us
    pallas_call x1, Pallas kernels, counts(): pl.pallas_call(counts_kernel, out_shape=jax.ShapeDtypeStruct((16, LANES),...  15.6 us
    all_to_all x1, waiting for transfers between devices, shards(): lax.all_to_all(residual.reshape(owners, rows, LANES), 'tm', split_axis=0,...  12.9 us
    all_to_all x1, starting transfers between devices, shards(): lax.all_to_all(residual.reshape(owners, rows, LANES), 'tm', split_axis=0,...  6.93 us
    unnamed x6, local copies, waits for them, and re-layouts  3.59 us
  transfers between devices with their start and end apart: 1, of which 1 were waited for; matrix products, arithmetic and copies ran while one was open for 0% of the time, Pallas kernels for 16%

profile of v1, /device:TPU:1, one launch (start us, length us, event | category | flops | bytes accessed | tf_op | source)
XLA Modules:
  0.0 98.1 jit_solution(12566995401344288945)
XLA Ops:
  0.6 22.6 %fit.1 = (f32[16,256]{1,0:T(8,128)}, f32[2048,128]{1,0:T(8,128)}) custom-call(s32[256]{0:T(256)} %wafer_ref.1, f32[256,1024]{1,0:T(8,128)} %data_ref.1, bf16[8,16,1024]{2,1,0:T(8,128)(2,1)} %templates_ref.1), custom_call_target="tpu_custom_call" | custom-call | tf_op jit(solution)/shard_map/fit/pallas_call | solution.py:143
  23.2 6.9 %all-to-all-start = ((f32[64,32,128]{2,1,0:T(8,128)}), f32[64,32,128]{2,1,0:T(8,128)S(1)}, u32[]{:S(2)}, u32[]{:S(2)}) async-start(f32[64,32,128]{2,1,0:T(8,128)} %bitcast.12), calls=%async_computation | async-start | bytes 2097152 | tf_op jit(solution)/shard_map/all_to_all | solution.py:427
  30.2 15.6 %counts.1.weight_ref = f32[16,128]{1,0:T(8,128)} custom-call(s32[4,65536]{1,0:T(4,128)} %tile_ref.3, s32[4,65536]{1,0:T(4,128)} %pixel_ref.3, f32[4]{0:T(128)} %white_ref.3), custom_call_target="tpu_custom_call" | custom-call | flops 10000000000 | bytes 2097152 | tf_op jit(solution)/shard_map/counts/pallas_call | solution.py:210
  45.8 12.9 %all-to-all-done = f32[64,32,128]{2,1,0:T(8,128)S(1)} async-done(((f32[64,32,128]{2,1,0:T(8,128)}), f32[64,32,128]{2,1,0:T(8,128)S(1)}, u32[]{:S(2)}, u32[]{:S(2)}) %all-to-all-start) | async-done | bytes 1048608 | tf_op jit(solution)/shard_map/all_to_all | solution.py:427
  58.7 0.0 copy-start
  58.7 1.0 copy-done
  59.7 0.0 copy-start.1
  59.7 34.6 %weigh.1 = (bf16[2048,128]{1,0:T(8,128)(2,1)}, f32[16,2,128]{2,1,0:T(2,128)}) custom-call(f32[4]{0:T(128)} %knee_ref.1, f32[4]{0:T(128)} %white_ref.3, s32[16]{0:T(128)} %order_ref.1, f32[2048,128]{1,0:T(8,128)} %bitcast.11, s32[4,65536]{1,0:T(4,128)} %tile_ref.3, s32[4,65536]{1,0:T(4,128)} %pixel_ref.3, f32[16,128]{1,0:T(8,128)} %counts.1.weight_ref, ...), custom_call_target="tpu_custom_call" | custom-call | tf_op jit(solution)/shard_map/weigh/pallas_call | solution.py:396
  94.2 0.7 slice.11
  94.9 0.1 constant_dynamic-slice_fusion
  95.0 0.5 slice_bitcast_fusion
  95.5 0.0 copy-done.1
  95.5 0.6 copy.24
  96.1 2.0 %copy.25 = bf16[4,65536]{1,0:T(4,128)(2,1)} copy(bf16[4,65536]{1,0:T(4,128)(2,1)} %bitcast.13) | data formatting | bytes 1048576
Async XLA Ops:
  23.2 35.5 %all-to-all-start = ((f32[64,32,128]{2,1,0:T(8,128)}), f32[64,32,128]{2,1,0:T(8,128)S(1)}, u32[]{:S(2)}, u32[]{:S(2)}) async-start(f32[64,32,128]{2,1,0:T(8,128)} %bitcast.12), calls=%async_computation | async-start | bytes 2097152 | tf_op jit(solution)/shard_map/all_to_all | solution.py:427
  58.7 1.0 copy-start
  59.7 35.8 %copy-start.1 = (f32[16,256]{1,0:T(8,128)S(1)}, f32[16,256]{1,0:T(8,128)}, u32[]{:S(2)}) copy-start(f32[16,256]{1,0:T(8,128)} %get-tuple-element.18) | copy-start | bytes 49156

commit v2 on v1

v2 whole, which is shorter than its diff:
```python
import functools
import math

import jax
import jax.numpy as jnp
import numpy as np
from jax import lax
from jax.experimental import pallas as pl
from jax.experimental.pallas import tpu as pltpu
from jax.sharding import PartitionSpec as P

PIX = 128
MODES = 16
LANES = 128
SIDE = 256
HALF = SIDE // 2
ROWS = HALF + 8
sample_rate = 200.0
f32 = jnp.float32
bf16 = jnp.bfloat16
MESH = pl.DeviceIdType.MESH
NT = (((1,), (1,)), ((), ()))
NN = (((1,), (0,)), ((), ()))


def mm(a, b, dims=NN):
    return lax.dot_general(a, b, dims, preferred_element_type=f32)


def split2(x):
    high = x.astype(bf16)
    low = (x - high.astype(f32)).astype(bf16)
    return high, low


def split3(x):
    high = x.astype(bf16)
    rest = x - high.astype(f32)
    mid = rest.astype(bf16)
    low = (rest - mid.astype(f32)).astype(bf16)
    return high, mid, low


def tables(chunks):
    full = SIDE * SIDE
    per = SIDE // chunks
    ramp = np.arange(SIDE)
    order = np.array([per * s + j for j in range(per) for s in range(chunks)])
    angle = 2.0 * np.pi / SIDE * (np.outer(ramp, ramp) % SIDE)
    cos, sin = np.cos(angle), np.sin(angle)
    first = np.concatenate([cos[:HALF], -sin[:HALF]], axis=0)
    first[HALF] = cos[HALF]
    second = np.block([[cos, -sin], [sin, cos]])
    weight = np.full((HALF,), 2.0)
    weight[0] = 1.0
    last = np.concatenate([cos[:, :HALF] * weight, -sin[:, :HALF] * weight], axis=1)
    last[:, HALF] = cos[:, HALF]
    k = np.arange(ROWS)
    turn = 2.0 * np.pi / full * np.outer(k, ramp)
    valid = (k <= HALF)[:, None]
    turn_cos, turn_sin = np.cos(turn) * valid, np.sin(turn) * valid
    bins = k[:, None] + SIDE * ramp[None, :]
    folded = np.minimum(bins, full - bins).astype(np.float32)
    frequency = folded * np.float32(sample_rate / full)
    squared = np.where(valid, frequency * frequency, np.float32(0)).astype(np.float32)

    def halves(a):
        a = a.astype(np.float32)
        high = a.astype(jnp.bfloat16)
        return high, (a - high.astype(np.float32)).astype(jnp.bfloat16)

    return (
        *halves(first[:, order]),
        *halves(second),
        *halves(last / full),
        turn_cos.astype(np.float32),
        turn_sin.astype(np.float32),
        squared,
    )


def three(left, right, dims=NN):
    return mm(left[0], right[0], dims) + mm(left[0], right[1], dims) + mm(left[1], right[0], dims)


CHUNK = 8192
f8 = jnp.float8_e4m3fn


def whole_kernel(
    sizes, scale, wafer_ref, knee_ref, white_ref, order_ref, data_ref, templates_ref, *refs
):
    x_size, z_size, det_size = sizes
    stored, refs = refs[:11], refs[11:]
    amps_ref, flat, maps_ref = refs[:3]
    held, refs = refs[3:14], refs[14:]
    (
        fetch_sem, left_ids, right_ids, parts, from_core, x_slots, z_slots, both, sent, got, comb, rows_out,
        tm_slots, det_slots, core_send, core_recv, x_send, x_recv, z_send, z_recv, move_send, move_recv,
        tm_send, tm_recv, det_send, det_recv,
    ) = refs
    tile_ref, pixel_ref = held[:2]
    first_high, first_low, second_high, second_low, last_high, last_low, turn_cos, turn_sin, squared_ref = held[2:]
    dets, samples = tile_ref.shape
    owners = x_size * z_size * 2
    tm = lax.axis_index("tm")
    det = lax.axis_index("det")
    core = tm % 2
    z = (tm // 2) % z_size
    x = tm // (2 * z_size)

    def index_of(x_at, z_at, core_at):
        return (x_at * z_size + z_at) * 2 + core_at

    other = index_of(x, z, 1 - core)
    x_peers = [index_of((x + k) % x_size, z, core) for k in range(1, x_size)]
    z_peers = [index_of(x, (z + k) % z_size, core) for k in range(1, z_size)]
    peers = [other] + x_peers + z_peers
    barrier = pltpu.get_barrier_semaphore()
    for peer in peers:
        pl.semaphore_signal(barrier, inc=1, device_id={"tm": peer}, device_id_type=MESH)
    for k in range(1, det_size):
        pl.semaphore_signal(barrier, inc=1, device_id={"det": (det + k) % det_size}, device_id_type=MESH)
    fetches = [
        pltpu.make_async_copy(stored[k], held[k], fetch_sem.at[k]) for k in range(len(stored))
    ]
    for fetch in fetches:
        fetch.start()

    run = data_ref.shape[0] // 2
    shapes = []
    for w in range(2):
        shape = templates_ref[wafer_ref[w * run]]
        shapes.append(shape)
        high, mid, low = split3(data_ref[w * run : (w + 1) * run, :])
        projected = mm(shape, high, NT) + mm(shape, mid, NT) + mm(shape, low, NT)
        gram = mm(shape, shape, NT)
        parts[w, 0:MODES, :] = projected
        pad = jnp.zeros((8, LANES - 2 * MODES), f32)
        parts[w, MODES : MODES + 8, :] = jnp.concatenate([gram[0:8], gram[8:16], pad], axis=1)

    pl.semaphore_wait(barrier, len(peers) + det_size - 1)
    copy = pltpu.make_async_remote_copy(
        src_ref=parts.at[1 - core], dst_ref=from_core, send_sem=core_send.at[0], recv_sem=core_recv.at[0],
        device_id={"tm": other}, device_id_type=MESH,
    )
    copy.start()

    def ids(turn, carry):
        span = pl.ds(pl.multiple_of(turn * CHUNK, CHUNK), CHUNK)
        tiles = tile_ref[:, span]
        pixels = pixel_ref[:, span]
        left_ids[:, span] = (tiles + 16 * (pixels >> 6)).astype(f32)
        right_ids[:, span] = (pixels & 63).astype(f32)
        return carry

    for fetch in fetches[:2]:
        fetch.wait()
    lax.fori_loop(0, samples // CHUNK, ids, 0)
    copy.wait()
    mine = parts[core] + from_core[...]

    one, zero = jnp.ones((), bf16), jnp.zeros((), bf16)

    def ramp(rows):
        return lax.broadcasted_iota(jnp.int32, (rows, CHUNK), 0).astype(f32).astype(bf16)

    def binned(d, total, value_of):
        def step(turn, total):
            span = pl.ds(pl.multiple_of(turn * CHUNK, CHUNK), CHUNK)
            left_id = left_ids[pl.ds(d, 1), span].astype(bf16)
            right_id = right_ids[pl.ds(d, 1), span].astype(bf16)
            left = jnp.where(left_id == ramp(32), value_of(turn), zero)
            right = jnp.where(right_id == ramp(64), one, zero).astype(f8)
            return total + mm(left, right, NT)

        return lax.fori_loop(0, samples // CHUNK, step, total)

    def count(d, total):
        inverse = (jnp.ones((1, 64), f32) / jnp.full((1, 64), white_ref[d], f32)).astype(bf16).astype(f32)
        return total + binned(d, jnp.zeros((32, 64), f32), lambda turn: one) * inverse

    def exchange(mine, slots, place, peers, send_sem, recv_sem, meanwhile):
        slots[place] = mine
        copies = []
        for k, peer in enumerate(peers):
            copy = pltpu.make_async_remote_copy(
                src_ref=slots.at[place], dst_ref=slots.at[place], send_sem=send_sem.at[k], recv_sem=recv_sem.at[k],
                device_id={"tm": peer}, device_id_type=MESH,
            )
            copy.start()
            copies.append(copy)
        result = meanwhile()
        for copy in copies:
            copy.wait()
        total = slots[0]
        for k in range(1, len(peers) + 1):
            total = total + slots[k]
        return total, result

    weight = jnp.zeros((32, 64), f32)
    mine, weight = exchange(mine, x_slots, x, x_peers, x_send, x_recv, lambda: count(0, weight))
    mine, weight = exchange(mine, z_slots, z, z_peers, z_send, z_recv, lambda: lax.fori_loop(1, 3, count, weight))
    both[core] = mine
    copy = pltpu.make_async_remote_copy(
        src_ref=both.at[core], dst_ref=both.at[core], send_sem=core_send.at[1], recv_sem=core_recv.at[1],
        device_id={"tm": other}, device_id_type=MESH,
    )
    copy.start()
    copy.wait()

    row = lax.broadcasted_iota(jnp.int32, (1, MODES, LANES), 1)
    for w in range(2):
        packed = both[w, MODES : MODES + 8, :]
        columns = []
        for k in range(MODES):
            top = jnp.broadcast_to(packed[:, k : k + 1], (8, LANES))
            low = jnp.broadcast_to(packed[:, MODES + k : MODES + k + 1], (8, LANES))
            columns.append(jnp.concatenate([top, low], axis=0))
        columns.append(both[w, 0:MODES, :])
        joined = jnp.stack(columns, axis=0)
        for c in range(MODES):
            factor = joined[0:1]
            pivot_row = joined[1:, c : c + 1, :] / factor[:, c : c + 1, :]
            joined = jnp.where(row == c, pivot_row, joined[1:] - factor * pivot_row)
        amps = joined[0]
        amps_ref[:, w * run : (w + 1) * run] = amps
        high, mid, low = split3(amps)
        left = jnp.concatenate([high, mid, low], axis=0)
        right = jnp.concatenate([shapes[w]] * 3, axis=0)
        fitted = lax.dot_general(left, right, (((0,), (0,)), ((), ())), preferred_element_type=f32)
        residual = data_ref[w * run : (w + 1) * run, :] - fitted
        tiles = residual.shape[1] // LANES
        for l in range(tiles):
            sent[pl.ds(w * run * tiles + l, run, stride=tiles), :] = residual[:, l * LANES : (l + 1) * LANES]

    piece = got.shape[1] // owners

    def move(d, carry):
        def one_peer(k, carry):
            peer = (tm + k) % owners
            pltpu.make_async_remote_copy(
                src_ref=sent.at[pl.ds((peer * dets + d) * piece, piece)], dst_ref=got.at[d, pl.ds(tm * piece, piece)],
                send_sem=move_send.at[d], recv_sem=move_recv.at[d], device_id={"tm": peer}, device_id_type=MESH,
            ).start()
            return carry

        lax.fori_loop(1, owners, one_peer, 0)
        got[d, pl.ds(pl.multiple_of(tm * piece, piece), piece), :] = sent[
            pl.ds(pl.multiple_of((tm * dets + d) * piece, piece), piece), :
        ]
        return carry

    lax.fori_loop(0, dets, move, 0)
    weight = count(dets - 1, weight)
    for fetch in fetches[2:]:
        fetch.wait()

    chunks = owners
    per = SIDE // chunks
    tiles = SIDE // LANES

    def weigh(d, total):
        arrived = pltpu.make_async_remote_copy(
            src_ref=got.at[d, pl.ds(0, (owners - 1) * piece)], dst_ref=got.at[d, pl.ds(0, (owners - 1) * piece)],
            send_sem=move_send.at[d], recv_sem=move_recv.at[d], device_id={"tm": other}, device_id_type=MESH,
        )
        arrived.wait()
        rows = []
        for j in range(per):
            rows.append(
                jnp.concatenate(
                    [got[d, pl.ds(j * tiles + h, chunks, stride=piece), :] for h in range(tiles)], axis=1
                )
            )
        signal = jnp.concatenate(rows, axis=0)
        spectrum = three((first_high[...], first_low[...]), split2(signal))
        real_y, imag_y, tail = spectrum[0:HALF], spectrum[HALF:], spectrum[HALF : HALF + 8]
        first_row = lax.broadcasted_iota(jnp.int32, (HALF, SIDE), 0) == 0
        imag_y = jnp.where(first_row, 0.0, imag_y)
        cos_main, sin_main = turn_cos[0:HALF, :], turn_sin[0:HALF, :]
        cos_tail, sin_tail = turn_cos[HALF:, :], turn_sin[HALF:, :]
        real_z = jnp.concatenate([real_y * cos_main + imag_y * sin_main, tail * cos_tail], axis=0)
        imag_z = jnp.concatenate([imag_y * cos_main - real_y * sin_main, -tail * sin_tail], axis=0)
        bins = three(
            split2(jnp.concatenate([real_z, imag_z], axis=1)), (second_high[...], second_low[...])
        )
        squared = squared_ref[...]
        knee = knee_ref[d]
        gain = squared / (white_ref[d] * (squared + knee * knee))
        bins = bins * jnp.concatenate([gain, gain], axis=1)
        back = three(split2(bins), (second_high[...], second_low[...]), NT)
        real_u, imag_u = back[:, 0:SIDE], back[:, SIDE:]
        real_w = real_u[0:HALF] * cos_main - imag_u[0:HALF] * sin_main
        imag_w = real_u[0:HALF] * sin_main + imag_u[0:HALF] * cos_main
        tail_w = (real_u[HALF:] * cos_tail - imag_u[HALF:] * sin_tail)[0:1]
        imag_w = jnp.where(first_row, jnp.broadcast_to(tail_w, (HALF, SIDE)), imag_w)
        joined = jnp.concatenate([real_w, imag_w], axis=0)
        output = three((last_high[...], last_low[...]), split2(joined))
        for h in range(tiles):
            part = output[:, h * LANES : (h + 1) * LANES]
            flat[pl.ds(h * dets + d, SIDE, stride=tiles * dets), :] = part
            rows_out[pl.ds(h, SIDE, stride=tiles), :] = part.astype(bf16).astype(f32)

        def value_of(turn):
            width = CHUNK // LANES
            values = rows_out[pl.ds(pl.multiple_of(turn * width, width), width), :].astype(bf16)
            return jnp.concatenate([values[l : l + 1, :] for l in range(width)], axis=1)

        return binned(d, total, value_of)

    sky = lax.fori_loop(0, dets, weigh, jnp.zeros((32, 64), f32))
    comb[0] = jnp.concatenate([sky[0:16], sky[16:32]], axis=1)
    comb[1] = jnp.concatenate([weight[0:16], weight[16:32]], axis=1)
    share = owners // 16
    ordered = maps_ref.shape[0]
    for r in range(ordered):
        tile = order_ref[r]
        maps_ref[r, 0:1, :] = comb[0, pl.ds(tile, 1), :]
        maps_ref[r, 1:2, :] = comb[1, pl.ds(tile, 1), :]

    def send(k, carry):
        peer = (tm + k) % owners
        pltpu.make_async_remote_copy(
            src_ref=maps_ref.at[peer // share], dst_ref=tm_slots.at[tm], send_sem=tm_send, recv_sem=tm_recv,
            device_id={"tm": peer}, device_id_type=MESH,
        ).start()
        return carry

    lax.fori_loop(1, owners, send, 0)
    tm_slots[tm] = maps_ref[tm // share]
    pltpu.make_async_remote_copy(
        src_ref=tm_slots.at[pl.ds(0, owners - 1)], dst_ref=tm_slots.at[pl.ds(0, owners - 1)],
        send_sem=tm_send, recv_sem=tm_recv, device_id={"tm": other}, device_id_type=MESH,
    ).wait()
    det_slots[det] = jnp.sum(tm_slots[...], axis=0)
    copies = []
    for k in range(1, det_size):
        copy = pltpu.make_async_remote_copy(
            src_ref=det_slots.at[det], dst_ref=det_slots.at[det], send_sem=det_send.at[k - 1],
            recv_sem=det_recv.at[k - 1], device_id={"det": (det + k) % det_size}, device_id_type=MESH,
        )
        copy.start()
        copies.append(copy)
    for copy in copies:
        copy.wait()
    total = det_slots[0]
    for k in range(1, det_size):
        total = total + det_slots[k]
    maps_ref[0] = total * scale


def whole(sizes, scale, owners, inputs):
    data, templates, wafer_of, knee_freq, white_level, tile_id, pixel_id, tile_order = inputs
    x_size, z_size, det_size = sizes
    rows, local = data.shape
    dets, samples = tile_id.shape
    stored = (tile_id, pixel_id) + tables(owners)
    vmem = pl.BlockSpec(memory_space=pltpu.VMEM)
    smem = pl.BlockSpec(memory_space=pltpu.SMEM)
    anywhere = pl.BlockSpec(memory_space=pl.ANY)
    part = (MODES + 8, LANES)
    dma = pltpu.SemaphoreType.DMA
    return pl.pallas_call(
        functools.partial(whole_kernel, sizes, scale),
        out_shape=(
            jax.ShapeDtypeStruct((MODES, rows), f32),
            jax.ShapeDtypeStruct((dets * samples // LANES, LANES), f32),
            jax.ShapeDtypeStruct((16, 2, LANES), f32),
        ),
        in_specs=[smem] * 4 + [vmem] * 2 + [anywhere] * len(stored),
        out_specs=[vmem] * 3,
        scratch_shapes=[pltpu.VMEM(a.shape, a.dtype) for a in stored]
        + [
            dma((len(stored),)),
            pltpu.VMEM((dets, samples), f32),
            pltpu.VMEM((dets, samples), f32),
            pltpu.VMEM((2,) + part, f32),
            pltpu.VMEM(part, f32),
            pltpu.VMEM((x_size,) + part, f32),
            pltpu.VMEM((z_size,) + part, f32),
            pltpu.VMEM((2,) + part, f32),
            pltpu.VMEM((rows * local // LANES, LANES), f32),
            pltpu.VMEM((dets, samples // LANES, LANES), f32),
            pltpu.VMEM((2, 16, LANES), f32),
            pltpu.VMEM((samples // LANES, LANES), f32),
            pltpu.VMEM((owners, 2, LANES), f32),
            pltpu.VMEM((det_size, 2, LANES), f32),
            dma((2,)),
            dma((2,)),
            dma((x_size - 1,)),
            dma((x_size - 1,)),
            dma((z_size - 1,)),
            dma((z_size - 1,)),
            dma((dets,)),
            dma((dets,)),
            dma,
            dma,
            dma((det_size - 1,)),
            dma((det_size - 1,)),
        ],
        compiler_params=pltpu.CompilerParams(collective_id=0, has_side_effects=True, vmem_limit_bytes=50 * 2**20),
        name="whole",
    )(wafer_of, knee_freq, white_level, tile_order, data, templates, *stored)


def shards(mesh, *inputs):
    owners = mesh.shape["tm"]
    det_size = mesh.shape["det"]
    dets, samples = inputs[5].shape
    cells = 16 * PIX
    scale = float(cells) / float(dets * owners * det_size * samples)
    fit_amps, flat, maps = whole((owners // 16, 8, det_size), scale, owners, inputs)
    weighted = flat.astype(bf16).reshape(samples // LANES, dets, LANES).transpose(1, 0, 2).reshape(dets, samples)
    share = cells // owners
    start = (lax.axis_index("tm") % (PIX // share)) * share
    own = lax.dynamic_slice(maps[0], (0, start), (2, share))
    return (fit_amps, weighted, own[0], own[1])


def solution(mesh):
    in_specs = (
        P("det", "tm"),
        P(None, None, "tm"),
        P("det"),
        P(("det", "tm")),
        P(("det", "tm")),
        P(("det", "tm"), None),
        P(("det", "tm"), None),
        P(),
    )
    out_specs = (P(None, "det"), P(("det", "tm"), None), P("tm"), P("tm"))
    return jax.shard_map(
        functools.partial(shards, mesh), mesh=mesh, in_specs=in_specs, out_specs=out_specs, check_vma=False
    )
```

time: 98.4 us -> 77 us (0.78)
  waiting for transfers between devices: 12.9 us -> 0 us
  Pallas kernels: 72.8 us -> 63.8 us
  starting transfers between devices: 6.93 us -> 0 us
  local copies, waits for them, and re-layouts: 4.86 us -> 11.2 us
    all_to_all x1 -> x0, waiting for transfers between devices: 12.9 us -> none  [shards(): lax.all_to_all(residual.reshape(owners, rows, LANES), 'tm', split_axis=0,...]
    pallas_call x3 -> x1, Pallas kernels: 72.8 us -> 63.8 us  [whole(): pl.pallas_call(functools.partial(whole_kernel, sizes, scale), out_shape=(...]
    unnamed x6 -> x29, local copies, waits for them, and re-layouts: 3.59 us -> 10.6 us
    all_to_all x1 -> x0, starting transfers between devices: 6.93 us -> none  [shards(): lax.all_to_all(residual.reshape(owners, rows, LANES), 'tm', split_axis=0,...]
  transfers between devices with their start and end apart: 1 -> 0, of which waited for: 1 -> 0; matrix products, arithmetic and copies ran while one was open for 0% -> 0% of each run, Pallas kernels for 16% -> 0%
where the time goes in v2:
time: 77 us; the launch traced here: 76.6 us
  Pallas kernels  63.8 us (83%)
  local copies, waits for them, and re-layouts  11.2 us (15%)
  other arithmetic  0.85 us (1%)
    pallas_call x1, Pallas kernels, whole(): pl.pallas_call(functools.partial(whole_kernel, sizes, scale), out_shape=(...  63.8 us
    unnamed x29, local copies, waits for them, and re-layouts  10.6 us

profile of v2, /device:TPU:1, one launch (start us, length us, event | category | flops | bytes accessed | tf_op | source)
XLA Modules:
  0.0 76.6 jit_solution(4970657883563132331)
XLA Ops:
  0.6 0.0 copy-start.13
  0.7 0.0 copy-start.10
  0.7 0.0 copy-start.11
  0.7 0.0 copy-start.12
  0.7 0.6 copy-done.13
  1.3 0.0 copy-done.10
  1.3 0.0 copy-done.11
  1.3 0.0 copy-done.12
  1.4 0.0 copy-start
  1.4 1.0 %copy-done = bf16[512,512]{1,0:T(8,128)(2,1)S(1)} copy-done((bf16[512,512]{1,0:T(8,128)(2,1)S(1)}, bf16[512,512]{1,0:T(8,128)(2,1)}, u32[]{:S(2)}) %copy-start) | copy-done | bytes 524312
  2.4 0.0 copy-start.1
  2.4 1.0 %copy-done.1 = bf16[512,512]{1,0:T(8,128)(2,1)S(1)} copy-done((bf16[512,512]{1,0:T(8,128)(2,1)S(1)}, bf16[512,512]{1,0:T(8,128)(2,1)}, u32[]{:S(2)}) %copy-start.1) | copy-done | bytes 524312
  3.4 0.0 copy-start.2
  3.4 0.9 %copy-done.2 = bf16[8,16,1024]{2,1,0:T(8,128)(2,1)S(1)} copy-done((bf16[8,16,1024]{2,1,0:T(8,128)(2,1)S(1)}, bf16[8,16,1024]{2,1,0:T(8,128)(2,1)}, u32[]{:S(2)}) %copy-start.2) | copy-done | bytes 262168
  4.4 0.0 copy-start.3
  4.4 0.9 %copy-done.3 = f32[136,256]{1,0:T(8,128)S(1)} copy-done((f32[136,256]{1,0:T(8,128)S(1)}, f32[136,256]{1,0:T(8,128)}, u32[]{:S(2)}) %copy-start.3) | copy-done | bytes 139288
  5.3 0.0 copy-start.4
  5.3 0.9 %copy-done.4 = f32[136,256]{1,0:T(8,128)S(1)} copy-done((f32[136,256]{1,0:T(8,128)S(1)}, f32[136,256]{1,0:T(8,128)}, u32[]{:S(2)}) %copy-start.4) | copy-done | bytes 139288
  6.2 0.0 copy-start.5
  6.2 0.9 %copy-done.5 = f32[136,256]{1,0:T(8,128)S(1)} copy-done((f32[136,256]{1,0:T(8,128)S(1)}, f32[136,256]{1,0:T(8,128)}, u32[]{:S(2)}) %copy-start.5) | copy-done | bytes 139288
  7.1 0.0 copy-start.6
  7.1 0.9 %copy-done.6 = bf16[256,256]{1,0:T(8,128)(2,1)S(1)} copy-done((bf16[256,256]{1,0:T(8,128)(2,1)S(1)}, bf16[256,256]{1,0:T(8,128)(2,1)}, u32[]{:S(2)}) %copy-start.6) | copy-done | bytes 131096
  8.0 0.0 copy-start.7
  8.0 0.9 %copy-done.7 = bf16[256,256]{1,0:T(8,128)(2,1)S(1)} copy-done((bf16[256,256]{1,0:T(8,128)(2,1)S(1)}, bf16[256,256]{1,0:T(8,128)(2,1)}, u32[]{:S(2)}) %copy-start.7) | copy-done | bytes 131096
  8.9 0.0 copy-start.8
  8.9 0.9 %copy-done.8 = bf16[256,256]{1,0:T(8,128)(2,1)S(1)} copy-done((bf16[256,256]{1,0:T(8,128)(2,1)S(1)}, bf16[256,256]{1,0:T(8,128)(2,1)}, u32[]{:S(2)}) %copy-start.8) | copy-done | bytes 131096
  9.8 0.0 copy-start.9
  9.8 0.9 %copy-done.9 = bf16[256,256]{1,0:T(8,128)(2,1)S(1)} copy-done((bf16[256,256]{1,0:T(8,128)(2,1)S(1)}, bf16[256,256]{1,0:T(8,128)(2,1)}, u32[]{:S(2)}) %copy-start.9) | copy-done | bytes 131096
  10.7 63.8 %whole.1 = (f32[16,256]{1,0:T(8,128)S(1)}, f32[2048,128]{1,0:T(8,128)S(1)}, f32[16,2,128]{2,1,0:T(2,128)S(1)}) custom-call(s32[256]{0:T(256)S(1)} %copy-done.10, f32[4]{0:T(128)S(1)} %copy-done.11, f32[4]{0:T(128)S(1)} %copy-done.12, s32[16]{0:T(128)S(1)} %copy-done.13, f32[256,1024]{1,0:T(8,128)} %data_ref.1, bf16[8,16,1024]{2,1,0:T(8,128)(2,1)S(1)} %copy-done.2, ...), custom_call_target="tpu_custom_call" | custom-call | tf_op jit(solution)/shard_map/whole/pallas_call | solution.py:364
  74.6 0.1 constant_dynamic-slice_fusion
  74.7 0.5 slice_bitcast_fusion
  75.2 0.8 %convert_element_type.3 = bf16[2048,128]{1,0:T(8,128)(2,1)} convert(f32[2048,128]{1,0:T(8,128)S(1)} %get-tuple-element.8) | non-fusion elementwise | flops 262144 | bytes 1572864 | tf_op jit(solution)/shard_map/convert_element_type | solution.py:414
  76.0 0.6 copy.23
  (1 shorter events, 0.0 us)
Async XLA Ops:
  0.6 0.7 copy-start.13
  0.7 0.7 copy-start.10
  0.7 0.7 copy-start.11
  0.7 0.7 copy-start.12
  1.4 1.0 %copy-start = (bf16[512,512]{1,0:T(8,128)(2,1)S(1)}, bf16[512,512]{1,0:T(8,128)(2,1)}, u32[]{:S(2)}) copy-start(bf16[512,512]{1,0:T(8,128)(2,1)} %constant.44.clone.refs_5_) | copy-start | bytes 1572868
  2.4 1.0 %copy-start.1 = (bf16[512,512]{1,0:T(8,128)(2,1)S(1)}, bf16[512,512]{1,0:T(8,128)(2,1)}, u32[]{:S(2)}) copy-start(bf16[512,512]{1,0:T(8,128)(2,1)} %constant.43.clone.refs_4_) | copy-start | bytes 1572868
  3.4 0.9 %copy-start.2 = (bf16[8,16,1024]{2,1,0:T(8,128)(2,1)S(1)}, bf16[8,16,1024]{2,1,0:T(8,128)(2,1)}, u32[]{:S(2)}) copy-start(bf16[8,16,1024]{2,1,0:T(8,128)(2,1)} %templates_ref.1) | copy-start | bytes 786436
  4.4 0.9 %copy-start.3 = (f32[136,256]{1,0:T(8,128)S(1)}, f32[136,256]{1,0:T(8,128)}, u32[]{:S(2)}) copy-start(f32[136,256]{1,0:T(8,128)} %constant.49.clone.refs_10_) | copy-start | bytes 417796
  5.3 0.9 %copy-start.4 = (f32[136,256]{1,0:T(8,128)S(1)}, f32[136,256]{1,0:T(8,128)}, u32[]{:S(2)}) copy-start(f32[136,256]{1,0:T(8,128)} %constant.48.clone.refs_9_) | copy-start | bytes 417796
  6.2 0.9 %copy-start.5 = (f32[136,256]{1,0:T(8,128)S(1)}, f32[136,256]{1,0:T(8,128)}, u32[]{:S(2)}) copy-start(f32[136,256]{1,0:T(8,128)} %constant.47.clone.refs_8_) | copy-start | bytes 417796
  7.1 0.9 %copy-start.6 = (bf16[256,256]{1,0:T(8,128)(2,1)S(1)}, bf16[256,256]{1,0:T(8,128)(2,1)}, u32[]{:S(2)}) copy-start(bf16[256,256]{1,0:T(8,128)(2,1)} %constant.46.clone.refs_7_) | copy-start | bytes 393220
  8.0 0.9 %copy-start.7 = (bf16[256,256]{1,0:T(8,128)(2,1)S(1)}, bf16[256,256]{1,0:T(8,128)(2,1)}, u32[]{:S(2)}) copy-start(bf16[256,256]{1,0:T(8,128)(2,1)} %constant.45.clone.refs_6_) | copy-start | bytes 393220
  8.9 0.9 %copy-start.8 = (bf16[256,256]{1,0:T(8,128)(2,1)S(1)}, bf16[256,256]{1,0:T(8,128)(2,1)}, u32[]{:S(2)}) copy-start(bf16[256,256]{1,0:T(8,128)(2,1)} %constant.42.clone.refs_3_) | copy-start | bytes 393220
  9.8 0.9 %copy-start.9 = (bf16[256,256]{1,0:T(8,128)(2,1)S(1)}, bf16[256,256]{1,0:T(8,128)(2,1)}, u32[]{:S(2)}) copy-start(bf16[256,256]{1,0:T(8,128)(2,1)} %constant.41.clone.refs_2_) | copy-start | bytes 393220

commit v3 on v2

--- a/solution.py
+++ b/solution.py
@@ -92,12 +92,12 @@
 ):
     x_size, z_size, det_size = sizes
     stored, refs = refs[:11], refs[11:]
-    amps_ref, flat, maps_ref = refs[:3]
+    amps_ref, flat_ref, maps_ref = refs[:3]
     held, refs = refs[3:14], refs[14:]
     (
-        fetch_sem, left_ids, right_ids, parts, from_core, x_slots, z_slots, both, sent, got, comb, rows_out,
-        tm_slots, det_slots, core_send, core_recv, x_send, x_recv, z_send, z_recv, move_send, move_recv,
-        tm_send, tm_recv, det_send, det_recv,
+        fetch_sem, left_ids, right_ids, parts, near_slots, z_slots, both, sent, got, flat, comb, rows_out,
+        tm_slots, det_slots, near_send, near_recv, z_send, z_recv, back_send, back_recv, move_send, move_recv,
+        tm_send, tm_recv, det_send, det_recv, flat_sem,
     ) = refs
     tile_ref, pixel_ref = held[:2]
     first_high, first_low, second_high, second_low, last_high, last_low, turn_cos, turn_sin, squared_ref = held[2:]
@@ -112,10 +112,13 @@
     def index_of(x_at, z_at, core_at):
         return (x_at * z_size + z_at) * 2 + core_at
 
-    other = index_of(x, z, 1 - core)
-    x_peers = [index_of((x + k) % x_size, z, core) for k in range(1, x_size)]
+    near_size = 2 * x_size
+    near = x * 2 + core
+    near_at = [(near + k) % near_size for k in range(1, near_size)]
+    near_peers = [index_of(at // 2, z, at % 2) for at in near_at]
     z_peers = [index_of(x, (z + k) % z_size, core) for k in range(1, z_size)]
-    peers = [other] + x_peers + z_peers
+    peers = near_peers + z_peers
+    other = near_peers[0]
     barrier = pltpu.get_barrier_semaphore()
     for peer in peers:
         pl.semaphore_signal(barrier, inc=1, device_id={"tm": peer}, device_id_type=MESH)
@@ -135,16 +138,22 @@
         high, mid, low = split3(data_ref[w * run : (w + 1) * run, :])
         projected = mm(shape, high, NT) + mm(shape, mid, NT) + mm(shape, low, NT)
         gram = mm(shape, shape, NT)
-        parts[w, 0:MODES, :] = projected
         pad = jnp.zeros((8, LANES - 2 * MODES), f32)
-        parts[w, MODES : MODES + 8, :] = jnp.concatenate([gram[0:8], gram[8:16], pad], axis=1)
+        parts[w * 4] = projected[0:8]
+        parts[w * 4 + 1] = projected[8:16]
+        parts[w * 4 + 2] = jnp.concatenate([gram[0:8], gram[8:16], pad], axis=1)
+        parts[w * 4 + 3] = jnp.zeros((8, LANES), f32)
 
     pl.semaphore_wait(barrier, len(peers) + det_size - 1)
-    copy = pltpu.make_async_remote_copy(
-        src_ref=parts.at[1 - core], dst_ref=from_core, send_sem=core_send.at[0], recv_sem=core_recv.at[0],
-        device_id={"tm": other}, device_id_type=MESH,
-    )
-    copy.start()
+    near_copies = []
+    for k in range(near_size - 1):
+        copy = pltpu.make_async_remote_copy(
+            src_ref=parts.at[near_at[k]], dst_ref=near_slots.at[near], send_sem=near_send.at[k],
+            recv_sem=near_recv.at[k], device_id={"tm": near_peers[k]}, device_id_type=MESH,
+        )
+        copy.start()
+        near_copies.append(copy)
+    near_slots[near] = parts[near]
 
     def ids(turn, carry):
         span = pl.ds(pl.multiple_of(turn * CHUNK, CHUNK), CHUNK)
@@ -157,9 +166,6 @@
     for fetch in fetches[:2]:
         fetch.wait()
     lax.fori_loop(0, samples // CHUNK, ids, 0)
-    copy.wait()
-    mine = parts[core] + from_core[...]
-
     one, zero = jnp.ones((), bf16), jnp.zeros((), bf16)
 
     def ramp(rows):
@@ -180,8 +186,7 @@
         inverse = (jnp.ones((1, 64), f32) / jnp.full((1, 64), white_ref[d], f32)).astype(bf16).astype(f32)
         return total + binned(d, jnp.zeros((32, 64), f32), lambda turn: one) * inverse
 
-    def exchange(mine, slots, place, peers, send_sem, recv_sem, meanwhile):
-        slots[place] = mine
+    def spread(slots, place, peers, send_sem, recv_sem):
         copies = []
         for k, peer in enumerate(peers):
             copy = pltpu.make_async_remote_copy(
@@ -190,34 +195,34 @@
             )
             copy.start()
             copies.append(copy)
-        result = meanwhile()
+        return copies
+
+    def gathered(slots, copies):
         for copy in copies:
             copy.wait()
         total = slots[0]
-        for k in range(1, len(peers) + 1):
+        for k in range(1, len(copies) + 1):
             total = total + slots[k]
-        return total, result
-
-    weight = jnp.zeros((32, 64), f32)
-    mine, weight = exchange(mine, x_slots, x, x_peers, x_send, x_recv, lambda: count(0, weight))
-    mine, weight = exchange(mine, z_slots, z, z_peers, z_send, z_recv, lambda: lax.fori_loop(1, 3, count, weight))
-    both[core] = mine
-    copy = pltpu.make_async_remote_copy(
-        src_ref=both.at[core], dst_ref=both.at[core], send_sem=core_send.at[1], recv_sem=core_recv.at[1],
-        device_id={"tm": other}, device_id_type=MESH,
-    )
-    copy.start()
-    copy.wait()
+        return total
+
+    weight = count(0, jnp.zeros((32, 64), f32))
+    z_slots[z] = gathered(near_slots, near_copies)
+    copies = spread(z_slots, z, z_peers, z_send, z_recv)
+    weight = count(1, weight)
+    both[near] = gathered(z_slots, copies)
+    copies = spread(both, near, near_peers, back_send, back_recv)
+    for copy in copies:
+        copy.wait()
 
     row = lax.broadcasted_iota(jnp.int32, (1, MODES, LANES), 1)
     for w in range(2):
-        packed = both[w, MODES : MODES + 8, :]
+        packed = both[w * 4 + 2]
         columns = []
         for k in range(MODES):
             top = jnp.broadcast_to(packed[:, k : k + 1], (8, LANES))
             low = jnp.broadcast_to(packed[:, MODES + k : MODES + k + 1], (8, LANES))
             columns.append(jnp.concatenate([top, low], axis=0))
-        columns.append(both[w, 0:MODES, :])
+        columns.append(jnp.concatenate([both[w * 4], both[w * 4 + 1]], axis=0))
         joined = jnp.stack(columns, axis=0)
         for c in range(MODES):
             factor = joined[0:1]
@@ -252,7 +257,7 @@
         return carry
 
     lax.fori_loop(0, dets, move, 0)
-    weight = count(dets - 1, weight)
+    weight = lax.fori_loop(2, dets, count, weight)
     for fetch in fetches[2:]:
         fetch.wait()
 
@@ -310,6 +315,8 @@
         return binned(d, total, value_of)
 
     sky = lax.fori_loop(0, dets, weigh, jnp.zeros((32, 64), f32))
+    flat_out = pltpu.make_async_copy(flat, flat_ref, flat_sem)
+    flat_out.start()
     comb[0] = jnp.concatenate([sky[0:16], sky[16:32]], axis=1)
     comb[1] = jnp.concatenate([weight[0:16], weight[16:32]], axis=1)
     share = owners // 16
@@ -348,6 +355,7 @@
     for k in range(1, det_size):
         total = total + det_slots[k]
     maps_ref[0] = total * scale
+    flat_out.wait()
 
 
 def whole(sizes, scale, owners, inputs):
@@ -358,8 +366,9 @@
     stored = (tile_id, pixel_id) + tables(owners)
     vmem = pl.BlockSpec(memory_space=pltpu.VMEM)
     smem = pl.BlockSpec(memory_space=pltpu.SMEM)
-    anywhere = pl.BlockSpec(memory_space=pl.ANY)
-    part = (MODES + 8, LANES)
+    anywhere = pl.BlockSpec(memory_space=pltpu.HBM)
+    part = (8, LANES)
+    near_size = 2 * x_size
     dma = pltpu.SemaphoreType.DMA
     return pl.pallas_call(
         functools.partial(whole_kernel, sizes, scale),
@@ -369,37 +378,38 @@
             jax.ShapeDtypeStruct((16, 2, LANES), f32),
         ),
         in_specs=[smem] * 4 + [vmem] * 2 + [anywhere] * len(stored),
-        out_specs=[vmem] * 3,
+        out_specs=[vmem, anywhere, vmem],
         scratch_shapes=[pltpu.VMEM(a.shape, a.dtype) for a in stored]
         + [
             dma((len(stored),)),
             pltpu.VMEM((dets, samples), f32),
             pltpu.VMEM((dets, samples), f32),
-            pltpu.VMEM((2,) + part, f32),
-            pltpu.VMEM(part, f32),
-            pltpu.VMEM((x_size,) + part, f32),
+            pltpu.VMEM((near_size,) + part, f32),
+            pltpu.VMEM((near_size,) + part, f32),
             pltpu.VMEM((z_size,) + part, f32),
-            pltpu.VMEM((2,) + part, f32),
+            pltpu.VMEM((near_size,) + part, f32),
             pltpu.VMEM((rows * local // LANES, LANES), f32),
             pltpu.VMEM((dets, samples // LANES, LANES), f32),
+            pltpu.VMEM((dets * samples // LANES, LANES), f32),
             pltpu.VMEM((2, 16, LANES), f32),
             pltpu.VMEM((samples // LANES, LANES), f32),
             pltpu.VMEM((owners, 2, LANES), f32),
             pltpu.VMEM((det_size, 2, LANES), f32),
-            dma((2,)),
-            dma((2,)),
-            dma((x_size - 1,)),
-            dma((x_size - 1,)),
+            dma((near_size - 1,)),
+            dma((near_size - 1,)),
             dma((z_size - 1,)),
             dma((z_size - 1,)),
+            dma((near_size - 1,)),
+            dma((near_size - 1,)),
             dma((dets,)),
             dma((dets,)),
             dma,
             dma,
             dma((det_size - 1,)),
             dma((det_size - 1,)),
+            dma,
         ],
-        compiler_params=pltpu.CompilerParams(collective_id=0, has_side_effects=True, vmem_limit_bytes=50 * 2**20),
+        compiler_params=pltpu.CompilerParams(collective_id=0, has_side_effects=True, vmem_limit_bytes=67043328),
         name="whole",
     )(wafer_of, knee_freq, white_level, tile_order, data, templates, *stored)
 

time: 77 us -> 69.6 us (0.904)
  local copies, waits for them, and re-layouts: 11.2 us -> 1.87 us
  other arithmetic: 0.85 us -> 2.08 us
  Pallas kernels: 63.8 us -> 64.8 us
    unnamed x29 -> x3, local copies, waits for them, and re-layouts: 10.6 us -> 0.61 us
    convert_element_type x1, other arithmetic: 0.85 us -> 2.08 us  [shards(): flat.astype(bf16).reshape(samples // LANES, dets, LANES).transpose(1, 0, 2)]
    pallas_call x1, Pallas kernels: 63.8 us -> 64.8 us  [whole(): pl.pallas_call(functools.partial(whole_kernel, sizes, scale), out_shape=(...]
where the time goes in v3:
time: 69.6 us; the launch traced here: 69.4 us
  Pallas kernels  64.8 us (93%)
  other arithmetic  2.08 us (3%)
  local copies, waits for them, and re-layouts  1.87 us (3%)
    pallas_call x1, Pallas kernels, whole(): pl.pallas_call(functools.partial(whole_kernel, sizes, scale), out_shape=(...  64.8 us
    convert_element_type x1, other arithmetic, shards(): flat.astype(bf16).reshape(samples // LANES, dets, LANES).transpose(1, 0, 2)  2.08 us

profile of v3, /device:TPU:1, one launch (start us, length us, event | category | flops | bytes accessed | tf_op | source)
XLA Modules:
  0.0 69.4 jit_solution(14824473040020419279)
XLA Ops:
  0.7 64.8 %whole.1 = (f32[16,256]{1,0:T(8,128)}, f32[2048,128]{1,0:T(8,128)}, f32[16,2,128]{2,1,0:T(2,128)}) custom-call(s32[256]{0:T(256)} %wafer_ref.1, f32[4]{0:T(128)} %knee_ref.1, f32[4]{0:T(128)} %white_ref.1, s32[16]{0:T(128)} %order_ref.1, f32[256,1024]{1,0:T(8,128)} %data_ref.1, bf16[8,16,1024]{2,1,0:T(8,128)(2,1)} %templates_ref.1, s32[4,65536]{1,0:T(4,128)} %refs_0_.1, ...), custom_call_target="tpu_custom_call" | custom-call | tf_op jit(solution)/shard_map/whole/pallas_call | solution.py:373
  65.5 0.7 slice.11
  66.1 0.1 constant_dynamic-slice_fusion
  66.2 0.5 slice_bitcast_fusion
  66.7 0.0 copy-start
  66.7 2.1 %convert_element_type.3 = bf16[2048,128]{1,0:T(8,128)(2,1)} convert(f32[2048,128]{1,0:T(8,128)} %get-tuple-element.8) | non-fusion elementwise | flops 262144 | bytes 1572864 | tf_op jit(solution)/shard_map/convert_element_type | solution.py:424
  68.8 0.0 copy-done
  68.8 0.6 copy.23
Async XLA Ops:
  66.7 2.1 %copy-start = (f32[16,256]{1,0:T(8,128)S(1)}, f32[16,256]{1,0:T(8,128)}, u32[]{:S(2)}) copy-start(f32[16,256]{1,0:T(8,128)} %get-tuple-element.16) | copy-start | bytes 49156

commit v4 on v3

--- a/solution.py
+++ b/solution.py
@@ -92,10 +92,10 @@
 ):
     x_size, z_size, det_size = sizes
     stored, refs = refs[:11], refs[11:]
-    amps_ref, flat_ref, maps_ref = refs[:3]
+    amps_ref, flat_ref, own_ref = refs[:3]
     held, refs = refs[3:14], refs[14:]
     (
-        fetch_sem, left_ids, right_ids, parts, near_slots, z_slots, both, sent, got, flat, comb, rows_out,
+        fetch_sem, left_ids, right_ids, hots, parts, near_slots, z_slots, both, sent, got, flat, rounded, comb, maps_ref, rows_out,
         tm_slots, det_slots, near_send, near_recv, z_send, z_recv, back_send, back_recv, move_send, move_recv,
         tm_send, tm_recv, det_send, det_recv, flat_sem,
     ) = refs
@@ -171,20 +171,20 @@
     def ramp(rows):
         return lax.broadcasted_iota(jnp.int32, (rows, CHUNK), 0).astype(f32).astype(bf16)
 
-    def binned(d, total, value_of):
+    def left_hot(d, span, value):
+        left_id = left_ids[pl.ds(d, 1), span].astype(bf16)
+        return jnp.where(left_id == ramp(32), value, zero)
+
+    def count(d, total):
         def step(turn, total):
             span = pl.ds(pl.multiple_of(turn * CHUNK, CHUNK), CHUNK)
-            left_id = left_ids[pl.ds(d, 1), span].astype(bf16)
             right_id = right_ids[pl.ds(d, 1), span].astype(bf16)
-            left = jnp.where(left_id == ramp(32), value_of(turn), zero)
             right = jnp.where(right_id == ramp(64), one, zero).astype(f8)
-            return total + mm(left, right, NT)
-
-        return lax.fori_loop(0, samples // CHUNK, step, total)
-
-    def count(d, total):
+            hots[d, :, span] = right
+            return total + mm(left_hot(d, span, one), right, NT)
+
         inverse = (jnp.ones((1, 64), f32) / jnp.full((1, 64), white_ref[d], f32)).astype(bf16).astype(f32)
-        return total + binned(d, jnp.zeros((32, 64), f32), lambda turn: one) * inverse
+        return total + lax.fori_loop(0, samples // CHUNK, step, jnp.zeros((32, 64), f32)) * inverse
 
     def spread(slots, place, peers, send_sem, recv_sem):
         copies = []
@@ -264,6 +264,11 @@
     chunks = owners
     per = SIDE // chunks
     tiles = SIDE // LANES
+
+    def turned(ref):
+        upper = jnp.concatenate([ref[0:SIDE, 0:SIDE], ref[SIDE:, 0:SIDE]], axis=1)
+        lower = jnp.concatenate([ref[0:SIDE, SIDE:], ref[SIDE:, SIDE:]], axis=1)
+        return jnp.concatenate([upper, lower], axis=0)
 
     def weigh(d, total):
         arrived = pltpu.make_async_remote_copy(
@@ -294,7 +299,7 @@
         knee = knee_ref[d]
         gain = squared / (white_ref[d] * (squared + knee * knee))
         bins = bins * jnp.concatenate([gain, gain], axis=1)
-        back = three(split2(bins), (second_high[...], second_low[...]), NT)
+        back = three(split2(bins), (turned(second_high), turned(second_low)))
         real_u, imag_u = back[:, 0:SIDE], back[:, SIDE:]
         real_w = real_u[0:HALF] * cos_main - imag_u[0:HALF] * sin_main
         imag_w = real_u[0:HALF] * sin_main + imag_u[0:HALF] * cos_main
@@ -307,15 +312,18 @@
             flat[pl.ds(h * dets + d, SIDE, stride=tiles * dets), :] = part
             rows_out[pl.ds(h, SIDE, stride=tiles), :] = part.astype(bf16).astype(f32)
 
-        def value_of(turn):
+        def step(turn, total):
+            span = pl.ds(pl.multiple_of(turn * CHUNK, CHUNK), CHUNK)
             width = CHUNK // LANES
             values = rows_out[pl.ds(pl.multiple_of(turn * width, width), width), :].astype(bf16)
-            return jnp.concatenate([values[l : l + 1, :] for l in range(width)], axis=1)
-
-        return binned(d, total, value_of)
+            value = jnp.concatenate([values[l : l + 1, :] for l in range(width)], axis=1)
+            return total + mm(left_hot(d, span, value), hots[d, :, span], NT)
+
+        return lax.fori_loop(0, samples // CHUNK, step, total)
 
     sky = lax.fori_loop(0, dets, weigh, jnp.zeros((32, 64), f32))
-    flat_out = pltpu.make_async_copy(flat, flat_ref, flat_sem)
+    rounded[...] = flat[...].astype(bf16)
+    flat_out = pltpu.make_async_copy(rounded, flat_ref, flat_sem)
     flat_out.start()
     comb[0] = jnp.concatenate([sky[0:16], sky[16:32]], axis=1)
     comb[1] = jnp.concatenate([weight[0:16], weight[16:32]], axis=1)
@@ -326,15 +334,28 @@
         maps_ref[r, 0:1, :] = comb[0, pl.ds(tile, 1), :]
         maps_ref[r, 1:2, :] = comb[1, pl.ds(tile, 1), :]
 
-    def send(k, carry):
-        peer = (tm + k) % owners
+    def send(dx, dz, dc):
+        peer = index_of((x + dx) % x_size, (z + dz) % z_size, (core + dc) % 2)
         pltpu.make_async_remote_copy(
             src_ref=maps_ref.at[peer // share], dst_ref=tm_slots.at[tm], send_sem=tm_send, recv_sem=tm_recv,
             device_id={"tm": peer}, device_id_type=MESH,
         ).start()
+
+    def far_first(size):
+        return sorted(range(size), key=lambda k: -min(k, size - k))
+
+    near_steps = [(dx, dc) for dx in far_first(x_size) for dc in (1, 0)]
+
+    def send_far(j, carry):
+        dz = z_size // 2 + (j + 1) // 2 * (2 * ((j + 1) % 2) - 1)
+        for dx, dc in near_steps:
+            send(dx, dz, dc)
         return carry
 
-    lax.fori_loop(1, owners, send, 0)
+    lax.fori_loop(0, z_size - 1, send_far, 0)
+    for dx, dc in near_steps:
+        if (dx, dc) != (0, 0):
+            send(dx, 0, dc)
     tm_slots[tm] = maps_ref[tm // share]
     pltpu.make_async_remote_copy(
         src_ref=tm_slots.at[pl.ds(0, owners - 1)], dst_ref=tm_slots.at[pl.ds(0, owners - 1)],
@@ -354,7 +375,12 @@
     total = det_slots[0]
     for k in range(1, det_size):
         total = total + det_slots[k]
-    maps_ref[0] = total * scale
+    total = total * scale
+    place = tm % share
+    own = total
+    for k in range(1, share):
+        own = jnp.where(place == k, pltpu.roll(total, LANES - k * (LANES // share), 1), own)
+    own_ref[...] = own
     flat_out.wait()
 
 
@@ -374,8 +400,8 @@
         functools.partial(whole_kernel, sizes, scale),
         out_shape=(
             jax.ShapeDtypeStruct((MODES, rows), f32),
-            jax.ShapeDtypeStruct((dets * samples // LANES, LANES), f32),
-            jax.ShapeDtypeStruct((16, 2, LANES), f32),
+            jax.ShapeDtypeStruct((dets * samples // LANES, LANES), bf16),
+            jax.ShapeDtypeStruct((2, LANES), f32),
         ),
         in_specs=[smem] * 4 + [vmem] * 2 + [anywhere] * len(stored),
         out_specs=[vmem, anywhere, vmem],
@@ -384,6 +410,7 @@
             dma((len(stored),)),
             pltpu.VMEM((dets, samples), f32),
             pltpu.VMEM((dets, samples), f32),
+            pltpu.VMEM((dets, 64, samples), f8),
             pltpu.VMEM((near_size,) + part, f32),
             pltpu.VMEM((near_size,) + part, f32),
             pltpu.VMEM((z_size,) + part, f32),
@@ -391,7 +418,9 @@
             pltpu.VMEM((rows * local // LANES, LANES), f32),
             pltpu.VMEM((dets, samples // LANES, LANES), f32),
             pltpu.VMEM((dets * samples // LANES, LANES), f32),
+            pltpu.VMEM((dets * samples // LANES, LANES), bf16),
             pltpu.VMEM((2, 16, LANES), f32),
+            pltpu.VMEM((16, 2, LANES), f32),
             pltpu.VMEM((samples // LANES, LANES), f32),
             pltpu.VMEM((owners, 2, LANES), f32),
             pltpu.VMEM((det_size, 2, LANES), f32),
@@ -414,6 +443,48 @@
     )(wafer_of, knee_freq, white_level, tile_order, data, templates, *stored)
 
 
+def finish_kernel(flat_ref, amps_ref, maps_ref, flat_out, amps_out, sky_out, weight_out, held, come, go):
+    count = come.shape[0]
+    rows = held.shape[0] // count
+    parts = [pl.ds(k * rows, rows) for k in range(count)]
+    comes = [pltpu.make_async_copy(flat_ref.at[parts[k]], held.at[parts[k]], come.at[k]) for k in range(count)]
+    goes = [pltpu.make_async_copy(held.at[parts[k]], flat_out.at[parts[k]], go.at[k]) for k in range(count)]
+    for copy in comes:
+        copy.start()
+    amps_out[...] = amps_ref[...]
+    share = sky_out.shape[1]
+    sky_out[...] = maps_ref[0:1, 0:share]
+    weight_out[...] = maps_ref[1:2, 0:share]
+    for k in range(count):
+        comes[k].wait()
+        goes[k].start()
+    for copy in goes:
+        copy.wait()
+
+
+def finish(fit_amps, flat, maps, share):
+    vmem = pl.BlockSpec(memory_space=pltpu.VMEM)
+    hbm = pl.BlockSpec(memory_space=pltpu.HBM)
+    return pl.pallas_call(
+        finish_kernel,
+        out_shape=(
+            jax.ShapeDtypeStruct(flat.shape, flat.dtype),
+            jax.ShapeDtypeStruct(fit_amps.shape, fit_amps.dtype),
+            jax.ShapeDtypeStruct((1, share), f32),
+            jax.ShapeDtypeStruct((1, share), f32),
+        ),
+        in_specs=[hbm, vmem, vmem],
+        out_specs=[hbm, vmem, vmem, vmem],
+        scratch_shapes=[
+            pltpu.VMEM(flat.shape, flat.dtype),
+            pltpu.SemaphoreType.DMA((4,)),
+            pltpu.SemaphoreType.DMA((4,)),
+        ],
+        compiler_params=pltpu.CompilerParams(vmem_limit_bytes=67043328),
+        name="finish",
+    )(flat, fit_amps, maps)
+
+
 def shards(mesh, *inputs):
     owners = mesh.shape["tm"]
     det_size = mesh.shape["det"]
@@ -421,11 +492,9 @@
     cells = 16 * PIX
     scale = float(cells) / float(dets * owners * det_size * samples)
     fit_amps, flat, maps = whole((owners // 16, 8, det_size), scale, owners, inputs)
-    weighted = flat.astype(bf16).reshape(samples // LANES, dets, LANES).transpose(1, 0, 2).reshape(dets, samples)
-    share = cells // owners
-    start = (lax.axis_index("tm") % (PIX // share)) * share
-    own = lax.dynamic_slice(maps[0], (0, start), (2, share))
-    return (fit_amps, weighted, own[0], own[1])
+    flat, fit_amps, sky, weight = finish(fit_amps, flat, maps, cells // owners)
+    weighted = flat.reshape(samples // LANES, dets, LANES).transpose(1, 0, 2).reshape(dets, samples)
+    return (fit_amps, weighted, sky.reshape(-1), weight.reshape(-1))
 
 
 def solution(mesh):

time: 69.6 us -> 68.2 us (0.980)
  Pallas kernels: 64.8 us -> 67.4 us
  other arithmetic: 2.08 us -> 0 us
  local copies, waits for them, and re-layouts: 1.87 us -> 0 us
    pallas_call x0 -> x1, Pallas kernels: none -> 3.15 us  [finish(): pl.pallas_call(finish_kernel, out_shape=(jax.ShapeDtypeStruct(flat.shape,...]
    convert_element_type x1 -> x0, other arithmetic: 2.08 us -> none  [shards(): flat.astype(bf16).reshape(samples // LANES, dets, LANES).transpose(1, 0, 2)]
where the time goes in v4:
time: 68.2 us; the launch traced here: 68 us
  Pallas kernels  67.4 us (99%)
    pallas_call x1, Pallas kernels, whole(): pl.pallas_call(functools.partial(whole_kernel, sizes, scale), out_shape=(...  64.2 us
    pallas_call x1, Pallas kernels, finish(): pl.pallas_call(finish_kernel, out_shape=(jax.ShapeDtypeStruct(flat.shape,...  3.15 us

profile of v4, /device:TPU:1, one launch (start us, length us, event | category | flops | bytes accessed | tf_op | source)
XLA Modules:
  0.0 68.0 jit_solution(11423039317884901523)
XLA Ops:
  0.6 64.2 %whole.1 = (f32[16,256]{1,0:T(8,128)}, bf16[2048,128]{1,0:T(8,128)(2,1)}, f32[2,128]{1,0:T(2,128)}) custom-call(s32[256]{0:T(256)} %wafer_ref.1, f32[4]{0:T(128)} %knee_ref.1, f32[4]{0:T(128)} %white_ref.1, s32[16]{0:T(128)} %order_ref.1, f32[256,1024]{1,0:T(8,128)} %data_ref.1, bf16[8,16,1024]{2,1,0:T(8,128)(2,1)} %templates_ref.1, s32[4,65536]{1,0:T(4,128)} %refs_0_.1, ...), custom_call_target="tpu_custom_call" | custom-call | tf_op jit(solution)/shard_map/whole/pallas_call | solution.py:399
  64.9 3.1 %finish.1 = (bf16[2048,128]{1,0:T(8,128)(2,1)}, f32[16,256]{1,0:T(8,128)}, f32[1,32]{1,0:T(1,128)}, f32[1,32]{1,0:T(1,128)}) custom-call(bf16[2048,128]{1,0:T(8,128)(2,1)} %get-tuple-element.11.flat_ref, f32[16,256]{1,0:T(8,128)} %get-tuple-element.12.amps_ref, f32[2,128]{1,0:T(2,128)} %get-tuple-element.13.maps_ref), custom_call_target="tpu_custom_call" | custom-call | tf_op jit(solution)/shard_map/finish/pallas_call | solution.py:468

commit v5 on v4

--- a/solution.py
+++ b/solution.py
@@ -88,14 +88,14 @@
 
 
 def whole_kernel(
-    sizes, scale, wafer_ref, knee_ref, white_ref, order_ref, data_ref, templates_ref, *refs
+    sizes, scale, wafer_ref, knee_ref, white_ref, order_ref, data_hbm, templates_ref, *refs
 ):
     x_size, z_size, det_size = sizes
     stored, refs = refs[:11], refs[11:]
     amps_ref, flat_ref, own_ref = refs[:3]
     held, refs = refs[3:14], refs[14:]
     (
-        fetch_sem, left_ids, right_ids, hots, parts, near_slots, z_slots, both, sent, got, flat, rounded, comb, maps_ref, rows_out,
+        data_ref, load_sem, fetch_sem, left_ids, right_ids, hots, gains, parts, near_slots, z_slots, both, sent, got, flat, rounded, comb, maps_ref, rows_out,
         tm_slots, det_slots, near_send, near_recv, z_send, z_recv, back_send, back_recv, move_send, move_recv,
         tm_send, tm_recv, det_send, det_recv, flat_sem,
     ) = refs
@@ -127,16 +127,23 @@
     fetches = [
         pltpu.make_async_copy(stored[k], held[k], fetch_sem.at[k]) for k in range(len(stored))
     ]
+
+    run = data_ref.shape[0] // 2
+    loads = [
+        pltpu.make_async_copy(data_hbm.at[pl.ds(w * run, run)], data_ref.at[pl.ds(w * run, run)], load_sem.at[w])
+        for w in range(2)
+    ]
+    for load in loads:
+        load.start()
     for fetch in fetches:
         fetch.start()
-
-    run = data_ref.shape[0] // 2
     shapes = []
     for w in range(2):
+        loads[w].wait()
         shape = templates_ref[wafer_ref[w * run]]
         shapes.append(shape)
-        high, mid, low = split3(data_ref[w * run : (w + 1) * run, :])
-        projected = mm(shape, high, NT) + mm(shape, mid, NT) + mm(shape, low, NT)
+        high, low = split2(data_ref[w * run : (w + 1) * run, :])
+        projected = mm(shape, high, NT) + mm(shape, low, NT)
         gram = mm(shape, shape, NT)
         pad = jnp.zeros((8, LANES - 2 * MODES), f32)
         parts[w * 4] = projected[0:8]
@@ -261,6 +268,13 @@
     for fetch in fetches[2:]:
         fetch.wait()
 
+    def gain_of(d, carry):
+        squared = squared_ref[...]
+        knee = knee_ref[d]
+        gains[d] = squared / (white_ref[d] * (squared + knee * knee))
+        return carry
+
+    lax.fori_loop(0, dets, gain_of, 0)
     chunks = owners
     per = SIDE // chunks
     tiles = SIDE // LANES
@@ -295,9 +309,7 @@
         bins = three(
             split2(jnp.concatenate([real_z, imag_z], axis=1)), (second_high[...], second_low[...])
         )
-        squared = squared_ref[...]
-        knee = knee_ref[d]
-        gain = squared / (white_ref[d] * (squared + knee * knee))
+        gain = gains[d]
         bins = bins * jnp.concatenate([gain, gain], axis=1)
         back = three(split2(bins), (turned(second_high), turned(second_low)))
         real_u, imag_u = back[:, 0:SIDE], back[:, SIDE:]
@@ -322,9 +334,6 @@
         return lax.fori_loop(0, samples // CHUNK, step, total)
 
     sky = lax.fori_loop(0, dets, weigh, jnp.zeros((32, 64), f32))
-    rounded[...] = flat[...].astype(bf16)
-    flat_out = pltpu.make_async_copy(rounded, flat_ref, flat_sem)
-    flat_out.start()
     comb[0] = jnp.concatenate([sky[0:16], sky[16:32]], axis=1)
     comb[1] = jnp.concatenate([weight[0:16], weight[16:32]], axis=1)
     share = owners // 16
@@ -357,6 +366,9 @@
         if (dx, dc) != (0, 0):
             send(dx, 0, dc)
     tm_slots[tm] = maps_ref[tm // share]
+    rounded[...] = flat[...].astype(bf16)
+    flat_out = pltpu.make_async_copy(rounded, flat_ref, flat_sem)
+    flat_out.start()
     pltpu.make_async_remote_copy(
         src_ref=tm_slots.at[pl.ds(0, owners - 1)], dst_ref=tm_slots.at[pl.ds(0, owners - 1)],
         send_sem=tm_send, recv_sem=tm_recv, device_id={"tm": other}, device_id_type=MESH,
@@ -403,14 +415,17 @@
             jax.ShapeDtypeStruct((dets * samples // LANES, LANES), bf16),
             jax.ShapeDtypeStruct((2, LANES), f32),
         ),
-        in_specs=[smem] * 4 + [vmem] * 2 + [anywhere] * len(stored),
+        in_specs=[smem] * 4 + [anywhere, vmem] + [anywhere] * len(stored),
         out_specs=[vmem, anywhere, vmem],
         scratch_shapes=[pltpu.VMEM(a.shape, a.dtype) for a in stored]
         + [
+            pltpu.VMEM(data.shape, f32),
+            dma((2,)),
             dma((len(stored),)),
             pltpu.VMEM((dets, samples), f32),
             pltpu.VMEM((dets, samples), f32),
             pltpu.VMEM((dets, 64, samples), f8),
+            pltpu.VMEM((dets, ROWS, SIDE), f32),
             pltpu.VMEM((near_size,) + part, f32),
             pltpu.VMEM((near_size,) + part, f32),
             pltpu.VMEM((z_size,) + part, f32),
@@ -443,28 +458,38 @@
     )(wafer_of, knee_freq, white_level, tile_order, data, templates, *stored)
 
 
-def finish_kernel(flat_ref, amps_ref, maps_ref, flat_out, amps_out, sky_out, weight_out, held, come, go):
-    count = come.shape[0]
-    rows = held.shape[0] // count
-    parts = [pl.ds(k * rows, rows) for k in range(count)]
-    comes = [pltpu.make_async_copy(flat_ref.at[parts[k]], held.at[parts[k]], come.at[k]) for k in range(count)]
-    goes = [pltpu.make_async_copy(held.at[parts[k]], flat_out.at[parts[k]], go.at[k]) for k in range(count)]
+def finish_kernel(
+    flat_ref, amps_ref, own_ref, flat_out, amps_out, sky_out, weight_out, held, amps, own, sky, weight, come, go
+):
+    parts = come.shape[0] - 2
+    rows = held.shape[0] // parts
+    cuts = [pl.ds(k * rows, rows) for k in range(parts)]
+    comes = [pltpu.make_async_copy(own_ref, own, come.at[parts]), pltpu.make_async_copy(amps_ref, amps, come.at[parts + 1])]
+    comes += [pltpu.make_async_copy(flat_ref.at[cuts[k]], held.at[cuts[k]], come.at[k]) for k in range(parts)]
+    goes = [pltpu.make_async_copy(held.at[cuts[k]], flat_out.at[cuts[k]], go.at[k]) for k in range(parts)]
     for copy in comes:
         copy.start()
-    amps_out[...] = amps_ref[...]
-    share = sky_out.shape[1]
-    sky_out[...] = maps_ref[0:1, 0:share]
-    weight_out[...] = maps_ref[1:2, 0:share]
-    for k in range(count):
-        comes[k].wait()
+    comes[0].wait()
+    share = sky.shape[1]
+    sky[...] = own[0:1, 0:share]
+    weight[...] = own[1:2, 0:share]
+    goes.append(pltpu.make_async_copy(sky, sky_out, go.at[parts]))
+    goes.append(pltpu.make_async_copy(weight, weight_out, go.at[parts + 1]))
+    for copy in goes[parts:]:
+        copy.start()
+    comes[1].wait()
+    goes.append(pltpu.make_async_copy(amps, amps_out, go.at[parts + 2]))
+    goes[-1].start()
+    for k in range(parts):
+        comes[2 + k].wait()
         goes[k].start()
     for copy in goes:
         copy.wait()
 
 
-def finish(fit_amps, flat, maps, share):
-    vmem = pl.BlockSpec(memory_space=pltpu.VMEM)
+def finish(fit_amps, flat, own, share):
     hbm = pl.BlockSpec(memory_space=pltpu.HBM)
+    parts = 4
     return pl.pallas_call(
         finish_kernel,
         out_shape=(
@@ -473,16 +498,20 @@
             jax.ShapeDtypeStruct((1, share), f32),
             jax.ShapeDtypeStruct((1, share), f32),
         ),
-        in_specs=[hbm, vmem, vmem],
-        out_specs=[hbm, vmem, vmem, vmem],
+        in_specs=[hbm] * 3,
+        out_specs=[hbm] * 4,
         scratch_shapes=[
             pltpu.VMEM(flat.shape, flat.dtype),
-            pltpu.SemaphoreType.DMA((4,)),
-            pltpu.SemaphoreType.DMA((4,)),
+            pltpu.VMEM(fit_amps.shape, f32),
+            pltpu.VMEM(own.shape, f32),
+            pltpu.VMEM((1, share), f32),
+            pltpu.VMEM((1, share), f32),
+            pltpu.SemaphoreType.DMA((parts + 2,)),
+            pltpu.SemaphoreType.DMA((parts + 3,)),
         ],
         compiler_params=pltpu.CompilerParams(vmem_limit_bytes=67043328),
         name="finish",
-    )(flat, fit_amps, maps)
+    )(flat, fit_amps, own)
 
 
 def shards(mesh, *inputs):

time: 68.2 us -> 67.4 us (0.988)
  Pallas kernels: 67.4 us -> 66.6 us
    pallas_call x1, Pallas kernels: 3.15 us -> 1.89 us  [finish(): pl.pallas_call(finish_kernel, out_shape=(jax.ShapeDtypeStruct(flat.shape,...]
where the time goes in v5:
time: 67.4 us; the launch traced here: 67.2 us
  Pallas kernels  66.6 us (99%)
    pallas_call x1, Pallas kernels, whole(): pl.pallas_call(functools.partial(whole_kernel, sizes, scale), out_shape=(...  64.7 us
    pallas_call x1, Pallas kernels, finish(): pl.pallas_call(finish_kernel, out_shape=(jax.ShapeDtypeStruct(flat.shape,...  1.89 us

profile of v5, /device:TPU:1, one launch (start us, length us, event | category | flops | bytes accessed | tf_op | source)
XLA Modules:
  0.0 67.2 jit_solution(17146618570008927236)
XLA Ops:
  0.6 64.7 %whole.1 = (f32[16,256]{1,0:T(8,128)}, bf16[2048,128]{1,0:T(8,128)(2,1)}, f32[2,128]{1,0:T(2,128)}) custom-call(s32[256]{0:T(256)} %wafer_ref.1, f32[4]{0:T(128)} %knee_ref.1, f32[4]{0:T(128)} %white_ref.1, s32[16]{0:T(128)} %order_ref.1, f32[256,1024]{1,0:T(8,128)} %data_hbm.1, bf16[8,16,1024]{2,1,0:T(8,128)(2,1)} %templates_ref.1, s32[4,65536]{1,0:T(4,128)} %refs_0_.1, ...), custom_call_target="tpu_custom_call" | custom-call | tf_op jit(solution)/shard_map/whole/pallas_call | solution.py:411
  65.4 1.9 %finish.1 = (bf16[2048,128]{1,0:T(8,128)(2,1)}, f32[16,256]{1,0:T(8,128)}, f32[1,32]{1,0:T(1,128)}, f32[1,32]{1,0:T(1,128)}) custom-call(bf16[2048,128]{1,0:T(8,128)(2,1)} %get-tuple-element.11.flat_ref, f32[16,256]{1,0:T(8,128)} %get-tuple-element.12.amps_ref, f32[2,128]{1,0:T(2,128)} %get-tuple-element.13.own_ref), custom_call_target="tpu_custom_call" | custom-call | tf_op jit(solution)/shard_map/finish/pallas_call | solution.py:493

commit v6 on v5

--- a/solution.py
+++ b/solution.py
@@ -83,7 +83,7 @@
     return mm(left[0], right[0], dims) + mm(left[0], right[1], dims) + mm(left[1], right[0], dims)
 
 
-CHUNK = 8192
+CHUNK = 16384
 f8 = jnp.float8_e4m3fn
 
 

time: 67.4 us -> 66.8 us (level)
  no operation moved by 1% of the time
where the time goes in v6:
time: 66.8 us; the launch traced here: 66.6 us
  Pallas kernels  66 us (99%)
    pallas_call x1, Pallas kernels, whole(): pl.pallas_call(functools.partial(whole_kernel, sizes, scale), out_shape=(...  64.1 us
    pallas_call x1, Pallas kernels, finish(): pl.pallas_call(finish_kernel, out_shape=(jax.ShapeDtypeStruct(flat.shape,...  1.89 us

profile of v6, /device:TPU:1, one launch (start us, length us, event | category | flops | bytes accessed | tf_op | source)
XLA Modules:
  0.0 66.6 jit_solution(1606845230575694867)
XLA Ops:
  0.6 64.1 %whole.1 = (f32[16,256]{1,0:T(8,128)}, bf16[2048,128]{1,0:T(8,128)(2,1)}, f32[2,128]{1,0:T(2,128)}) custom-call(s32[256]{0:T(256)} %wafer_ref.1, f32[4]{0:T(128)} %knee_ref.1, f32[4]{0:T(128)} %white_ref.1, s32[16]{0:T(128)} %order_ref.1, f32[256,1024]{1,0:T(8,128)} %data_hbm.1, bf16[8,16,1024]{2,1,0:T(8,128)(2,1)} %templates_ref.1, s32[4,65536]{1,0:T(4,128)} %refs_0_.1, ...), custom_call_target="tpu_custom_call" | custom-call | tf_op jit(solution)/shard_map/whole/pallas_call | solution.py:411
  64.8 1.9 %finish.1 = (bf16[2048,128]{1,0:T(8,128)(2,1)}, f32[16,256]{1,0:T(8,128)}, f32[1,32]{1,0:T(1,128)}, f32[1,32]{1,0:T(1,128)}) custom-call(bf16[2048,128]{1,0:T(8,128)(2,1)} %get-tuple-element.11.flat_ref, f32[16,256]{1,0:T(8,128)} %get-tuple-element.12.amps_ref, f32[2,128]{1,0:T(2,128)} %get-tuple-element.13.own_ref), custom_call_target="tpu_custom_call" | custom-call | tf_op jit(solution)/shard_map/finish/pallas_call | solution.py:493
